TPU v7x, 8 devices: a whole 2x2x1 slice. The times are simulated.
8 devices in a mesh: batch: 1 (over z), time: 2 (over y), region: 4 (over x, core).
Axes of the slice: x: 2, y: 2, z: 1, core: 2. Of those that a mesh axis runs over, the one named last changes fastest.
Arguments:
- patches: bfloat16 [2048, 1536], P(('batch', 'time', 'region'))
- enc_pos: bfloat16 [2048, 1280], P(('batch', 'time', 'region'))
- vis_mask: int32 [2048], P(('batch', 'time', 'region'))
- dec_pos: bfloat16 [2048, 512], P(('batch', 'time', 'region'))
- w_embed: bfloat16 [1536, 1280], replicated
- b_embed: float32 [1280], replicated
- enc_vec: float32 [2, 12, 1280], replicated
- enc_wqkv: bfloat16 [2, 1280, 3, 16, 80], replicated
- enc_wo: bfloat16 [2, 16, 80, 1280], replicated
- enc_w1: bfloat16 [2, 1280, 5120], replicated
- enc_w2: bfloat16 [2, 5120, 1280], replicated
- enc_final: float32 [2, 1280], replicated
- w_dec_in: bfloat16 [1280, 512], replicated
- mask_token: bfloat16 [512], replicated
- dec_vec: float32 [2, 12, 512], replicated
- dec_wqkv: bfloat16 [2, 512, 3, 16, 32], replicated
- dec_wo: bfloat16 [2, 16, 32, 512], replicated
- dec_w1: bfloat16 [2, 512, 2048], replicated
- dec_w2: bfloat16 [2, 2048, 512], replicated
- dec_final: float32 [2, 512], replicated
- w_out: bfloat16 [512, 1536], replicated
Outputs:
- output: float32 [2048, 1536], P(('batch', 'time', 'region'))
All inputs are finite; a program needn't handle non-finite values.
Results may differ from a plain program's by a relative error of at most 0.0172449.
Values are sent between devices in bfloat16 or wider.
A program may use at most 1 GiB of HBM per device.

v0:
```python
import functools
import jax
import jax.numpy as jnp
from jax import lax
from jax.sharding import PartitionSpec as P

KEEP_DIV = 8
LN_EPS = 1e-6
GROUP_AXES = ("time", "region")
TOKEN_AXES = ("batch", "time", "region")


def layer_norm(hidden, ln_gain, ln_shift):
    hid_f32 = hidden.astype(jnp.float32)
    mean_val = jnp.mean(hid_f32, axis=-1, keepdims=True)
    centered = hid_f32 - mean_val
    variance = jnp.mean(centered * centered, axis=-1, keepdims=True)
    return centered * lax.rsqrt(variance + LN_EPS) * ln_gain + ln_shift


def attend(query_rows, key_rows, value_rows, key_bias):
    head_dim = query_rows.shape[-1]
    scores = jnp.einsum("qhd,khd->hqk", query_rows, key_rows, preferred_element_type=jnp.float32) * (head_dim ** -0.5)
    if key_bias is not None:
        scores = scores + key_bias
    attn_probs = jax.nn.softmax(scores, axis=-1).astype(jnp.bfloat16)
    return jnp.einsum("hqk,khd->qhd", attn_probs, value_rows, preferred_element_type=jnp.float32).astype(jnp.bfloat16)


def run_block(hidden, vec_rows, w_qkv, w_o, w_one, w_two, gather_rows, key_bias):
    head_count, head_dim = w_qkv.shape[2], w_qkv.shape[3]
    normed = layer_norm(hidden, vec_rows[0], vec_rows[1]).astype(jnp.bfloat16)
    qkv_bias = jnp.stack([vec_rows[4], jnp.zeros_like(vec_rows[4]), vec_rows[5]]).reshape(1, 3, head_count, head_dim)
    qkv_rows = (jnp.einsum("nd,dche->nche", normed, w_qkv, preferred_element_type=jnp.float32) + qkv_bias).astype(jnp.bfloat16)
    key_rows = gather_rows(qkv_rows[:, 1])
    value_rows = gather_rows(qkv_rows[:, 2])
    attended = attend(qkv_rows[:, 0], key_rows, value_rows, key_bias)
    residual = (hidden.astype(jnp.float32) + jnp.einsum("nhe,hed->nd", attended, w_o, preferred_element_type=jnp.float32) + vec_rows[6]).astype(jnp.bfloat16)
    normed_mlp = layer_norm(residual, vec_rows[2], vec_rows[3]).astype(jnp.bfloat16)
    mlp_hidden = jax.nn.gelu(jnp.dot(normed_mlp, w_one, preferred_element_type=jnp.float32) + vec_rows[8:12].reshape(-1), approximate=False).astype(jnp.bfloat16)
    return (residual.astype(jnp.float32) + jnp.dot(mlp_hidden, w_two, preferred_element_type=jnp.float32) + vec_rows[7]).astype(jnp.bfloat16)


def solution(mesh):
    regions = mesh.shape["region"]
    skew_factor = min(4, regions)
    gather_group = functools.partial(lax.all_gather, axis_name=GROUP_AXES, axis=0, tiled=True)

    def local_step(patches, enc_pos, vis_mask, dec_pos, w_embed, b_embed, enc_vec, enc_wqkv, enc_wo, enc_w1, enc_w2, enc_final, w_dec_in, mask_token, dec_vec, dec_wqkv, dec_wo, dec_w1, dec_w2, dec_final, w_out):
        tokens_dev = patches.shape[0]
        vis_dev = tokens_dev // KEEP_DIV
        cap_rows = skew_factor * vis_dev
        enc_width = w_embed.shape[1]
        dec_width = w_dec_in.shape[1]
        region_pos = lax.axis_index("region")
        own_count = jnp.sum(vis_mask)
        counts = lax.all_gather(own_count[None], "region", axis=0, tiled=True)
        starts = jnp.cumsum(counts) - counts
        offset = starts[region_pos]
        slot_ids = jnp.arange(cap_rows, dtype=jnp.int32)
        local_rank = jnp.cumsum(vis_mask) - 1
        selector = ((local_rank[None, :] == slot_ids[:, None]) & (vis_mask[None, :] == 1)).astype(jnp.bfloat16)
        picked_patch = jnp.dot(selector, patches, preferred_element_type=jnp.float32).astype(jnp.bfloat16)
        picked_pos = jnp.dot(selector, enc_pos, preferred_element_type=jnp.float32)
        embedded = jnp.dot(picked_patch, w_embed, preferred_element_type=jnp.float32) + b_embed + picked_pos
        embedded = jnp.where((slot_ids < own_count)[:, None], embedded, 0.0).astype(jnp.bfloat16)
        rank_space = lax.dynamic_update_slice(jnp.zeros((regions * vis_dev + cap_rows, enc_width), jnp.bfloat16), embedded, (offset, 0))
        send_rows = rank_space[: regions * vis_dev].reshape(regions, vis_dev, enc_width)
        received = lax.all_to_all(send_rows, "region", 0, 0, tiled=True)
        hidden = jnp.sum(received, axis=0)
        for layer_idx in range(enc_vec.shape[0]):
            hidden = run_block(hidden, enc_vec[layer_idx], enc_wqkv[layer_idx], enc_wo[layer_idx], enc_w1[layer_idx], enc_w2[layer_idx], gather_group, None)
        latent = jnp.dot(layer_norm(hidden, enc_final[0], enc_final[1]).astype(jnp.bfloat16), w_dec_in, preferred_element_type=jnp.float32).astype(jnp.bfloat16)
        my_ranks = region_pos * vis_dev + jnp.arange(vis_dev, dtype=jnp.int32)
        from_source = (my_ranks[None, :] >= starts[:, None]) & (my_ranks[None, :] < (starts + counts)[:, None])
        back_rows = jnp.where(from_source[:, :, None], latent[None], jnp.zeros((), jnp.bfloat16))
        returned = lax.all_to_all(back_rows, "region", 0, 0, tiled=True)
        return_space = jnp.concatenate([returned.reshape(regions * vis_dev, dec_width), jnp.zeros((cap_rows, dec_width), jnp.bfloat16)], axis=0)
        own_latent = lax.dynamic_slice(return_space, (offset, 0), (cap_rows, dec_width))
        placed = jnp.einsum("ct,cd->td", selector, own_latent, preferred_element_type=jnp.float32)
        hidden = (jnp.where(vis_mask[:, None] == 1, placed, mask_token.astype(jnp.float32)) + dec_pos.astype(jnp.float32)).astype(jnp.bfloat16)
        for layer_idx in range(dec_vec.shape[0]):
            hidden = run_block(hidden, dec_vec[layer_idx], dec_wqkv[layer_idx], dec_wo[layer_idx], dec_w1[layer_idx], dec_w2[layer_idx], gather_group, None)
        return jnp.dot(layer_norm(hidden, dec_final[0], dec_final[1]).astype(jnp.bfloat16), w_out, preferred_element_type=jnp.float32)

    token_rows = P(TOKEN_AXES, None)
    token_flags = P(TOKEN_AXES)
    replicated = P()
    in_specs = (token_rows, token_rows, token_flags, token_rows) + (replicated,) * 17
    return jax.shard_map(local_step, mesh=mesh, in_specs=in_specs, out_specs=token_rows, check_vma=False)
```

profile of v0, /device:TPU:0, one launch (start us, length us, event | category | flops | bytes accessed | tf_op | source)
XLA Modules:
  0.0 333.0 jit_solution(5750809198109501373)
XLA Ops:
  6.5 0.8 broadcast_compare_fusion
  7.3 1.3 reduce_sum.237
  8.7 0.6 iota_compare_fusion.1
  9.3 1.3 dynamic-slice
  10.6 1.4 dynamic-update-slice
  12.1 6.8 %all-reduce.1 = s32[4]{0:T(128)S(1)} all-reduce(s32[4]{0:T(128)S(1)} %dynamic-update-slice), channel_id=1, replica_groups=mesh['batch'=1,'time'=2,'region'=4] {'region'}, use_global_device_ids=true, to_apply=%add.1 | all-reduce | flops 4 | bytes 32
  19.0 0.6 dynamic_slice.6
  20.9 1.0 reduce-window.19
  22.9 3.3 convolution_add_fusion.3
  26.5 2.0 dynamic_update_slice.3
  28.5 0.7 slice.361
  29.3 3.5 %all-to-all-start = ((bf16[4,32,1280]{2,1,0:T(8,128)(2,1)}), bf16[4,32,1280]{2,1,0:T(8,128)(2,1)S(1)}, u32[]{:S(2)}, u32[]{:S(2)}) async-start(bf16[4,32,1280]{2,1,0:T(8,128)(2,1)} %bitcast.7), calls=%async_computation | async-start | bytes 655360 | tf_op jit(solution)/shard_map/all_to_all | solution.py:69
  32.7 0.8 slice_reduce_fusion.4
  33.6 0.6 fusion.610
  34.2 1.2 fusion.611
  35.5 3.4 %fusion.605 = (bf16[1,512,3,16,32]{1,4,3,2,0:T(8,128)(2,1)S(1)}, bf16[1,512,3,16,32]{1,4,3,2,0:T(8,128)(2,1)}) fusion(bf16[2,512,3,16,32]{1,4,3,2,0:T(8,128)(2,1)} %param.36), kind=kLoop, calls=%fused_computation.606 | loop fusion | bytes 6291456 | tf_op jit(solution)/shard_map/slice | solution.py:83
  38.8 0.6 compare_and_fusion
  39.4 0.6 slice_reduce_fusion.1
  40.4 0.7 stack.39
  41.0 0.7 stack.41
  41.7 0.7 stack.43
  42.4 0.7 stack.44
  43.1 0.5 copy-done.38
  43.6 0.7 maximum_bitcast_fusion.1
  44.7 7.8 %fusion.161 = bf16[32,3,16,80]{3,0,2,1:T(8,128)(2,1)S(1)} fusion(bf16[2,1280,3,16,80]{1,4,3,2,0:T(8,128)(2,1)} %param.28, f32[3,16,80]{2,1,0:T(8,128)} %get-tuple-element.62, bf16[32,1280]{1,0:T(8,128)(2,1)S(1)} %reduce_sum.238, f32[1280]{0:T(1024)} %get-tuple-element.18, f32[1280]{0:T(1024)} %get-tuple-element.19, f32[32]{0:T(128)S(1)} %add_rsqrt_fusion.9, ...), kind=kOutput, calls=%fused_computation.132 | convolution fusion | flops 315064320 | bytes 10199296 | tf_op jit(solution)/shard_map/nd,dche->nche/dot_general | solution.py:34
  52.5 17.2 %all-gather.1 = bf16[256,1,16,80]{3,0,2,1:T(8,128)(2,1)S(1)} all-gather(bf16[32,1,16,80]{3,0,2,1:T(8,128)(2,1)S(1)} %get-tuple-element.35), channel_id=3, replica_groups=mesh['batch'=1,'time'=2,'region'=4] {'time','region'}, dimensions={0}, use_global_device_ids=true | all-gather | bytes 737280 | tf_op jit(solution)/shard_map/all_gather | solution.py:35
  70.2 0.8 copy-done.4
  71.3 16.1 %all-gather = bf16[256,1,16,80]{3,0,2,1:T(8,128)(2,1)} all-gather(bf16[32,1,16,80]{3,0,2,1:T(8,128)(2,1)S(1)} %get-tuple-element.36), channel_id=2, replica_groups=mesh['batch'=1,'time'=2,'region'=4] {'time','region'}, dimensions={0}, use_global_device_ids=true | all-gather | bytes 737280 | tf_op jit(solution)/shard_map/all_gather | solution.py:36
  87.4 3.9 %fusion.615 = (f32[32]{0:T(128)S(1)}, f32[32,1280]{1,0:T(8,128)S(1)}) fusion(f32[1280]{0:T(1024)S(1)} %copy-done.34, bf16[2,16,80,1280]{3,2,1,0:T(8,128)(2,1)} %param.29, bf16[256,1,16,80]{3,0,2,1:T(8,128)(2,1)} %all-gather, f32[16,32]{1,0:T(8,128)S(1)} %fusion.614, f32[16,32,256]{2,1,0:T(8,128)} %copy-done.4, bf16[32,1280]{1,0:T(8,128)(2,1)S(1)} %reduce_sum.238), kind=kOutput, calls=%fused_computation.616 | convolution fusion | flops 126509792 | bytes 5627008 | tf_op jit(solution)/shard_map/nhe,hed->nd/dot_general | solution.py:38
  91.6 11.6 %fusion.618 = (f32[32]{0:T(128)S(1)}, f32[32,1280]{1,0:T(8,128)S(1)}) fusion(f32[1280]{0:T(1024)} %get-tuple-element.12, f32[32,1280]{1,0:T(8,128)S(1)} %get-tuple-element.64, bf16[2,5120,1280]{2,1,0:T(8,128)(2,1)} %param.31, bf16[2,1280,5120]{2,1,0:T(8,128)(2,1)} %param.30, f32[5120]{0:T(1024)} %bitcast.376, f32[1280]{0:T(1024)} %get-tuple-element.13, ...), kind=kOutput, calls=%fused_computation.617 | convolution fusion | flops 850083840 | bytes 26752128 | tf_op jit(solution)/shard_map/dot_general | solution.py:41
  103.4 7.7 %fusion.158 = bf16[32,3,16,80]{3,0,2,1:T(8,128)(2,1)S(1)} fusion(bf16[2,1280,3,16,80]{1,4,3,2,0:T(8,128)(2,1)} %param.28, f32[3,16,80]{2,1,0:T(8,128)S(1)} %copy-done.15, f32[32,1280]{1,0:T(8,128)S(1)} %get-tuple-element.66, f32[1280]{0:T(1024)S(1)} %copy-done.32, f32[1280]{0:T(1024)S(1)} %copy-done.33, f32[32]{0:T(128)S(1)} %add_rsqrt_fusion.7, ...), kind=kOutput, calls=%fused_computation.131 | convolution fusion | flops 315023360 | bytes 10265856 | tf_op jit(solution)/shard_map/nd,dche->nche/dot_general | solution.py:34
  111.2 15.7 %all-gather.3 = bf16[256,1,16,80]{3,0,2,1:T(8,128)(2,1)S(1)} all-gather(bf16[32,1,16,80]{3,0,2,1:T(8,128)(2,1)S(1)} %get-tuple-element.33), channel_id=5, replica_groups=mesh['batch'=1,'time'=2,'region'=4] {'time','region'}, dimensions={0}, use_global_device_ids=true | all-gather | bytes 737280 | tf_op jit(solution)/shard_map/all_gather | solution.py:35
  126.8 0.5 convolution_multiply_fusion
  127.3 0.8 copy-done.5
  128.4 15.7 %all-gather.2 = bf16[256,1,16,80]{3,0,2,1:T(8,128)(2,1)} all-gather(bf16[32,1,16,80]{3,0,2,1:T(8,128)(2,1)S(1)} %get-tuple-element.34), channel_id=4, replica_groups=mesh['batch'=1,'time'=2,'region'=4] {'time','region'}, dimensions={0}, use_global_device_ids=true | all-gather | bytes 737280 | tf_op jit(solution)/shard_map/all_gather | solution.py:36
  144.1 4.0 %fusion.622 = (f32[32]{0:T(128)S(1)}, f32[32,1280]{1,0:T(8,128)S(1)}) fusion(f32[1280]{0:T(1024)S(1)} %copy-done.31, f32[32,1280]{1,0:T(8,128)S(1)} %get-tuple-element.66, bf16[2,16,80,1280]{3,2,1,0:T(8,128)(2,1)} %param.29, bf16[256,1,16,80]{3,0,2,1:T(8,128)(2,1)} %all-gather.2, f32[16,32]{1,0:T(8,128)S(1)} %fusion.621, f32[16,32,256]{2,1,0:T(8,128)} %copy-done.5), kind=kOutput, calls=%fused_computation.619 | convolution fusion | flops 126468832 | bytes 5708928 | tf_op jit(solution)/shard_map/nhe,hed->nd/dot_general | solution.py:38
  148.3 11.5 %fusion.625 = (f32[32]{0:T(128)S(1)}, f32[32,1280]{1,0:T(8,128)S(1)}) fusion(f32[1280]{0:T(1024)S(1)} %copy-done.30, f32[32,1280]{1,0:T(8,128)S(1)} %get-tuple-element.68, bf16[2,5120,1280]{2,1,0:T(8,128)(2,1)} %param.31, bf16[2,1280,5120]{2,1,0:T(8,128)(2,1)} %param.30, f32[5120]{0:T(1024)S(1)} %bitcast.375, f32[1280]{0:T(1024)S(1)} %copy-done.29, ...), kind=kOutput, calls=%fused_computation.620 | convolution fusion | flops 850083840 | bytes 26752128 | tf_op jit(solution)/shard_map/dot_general | solution.py:41
  160.1 1.7 convolution_convert_fusion.3
  161.8 0.7 broadcast_select_fusion
  162.5 3.3 all-to-all-start.1
  165.9 0.6 all-gather.15.cloned.1.call-start
  166.6 3.7 %all-to-all-done.1 = bf16[4,32,512]{2,1,0:T(8,128)(2,1)S(1)} async-done(((bf16[4,32,512]{2,1,0:T(8,128)(2,1)}), bf16[4,32,512]{2,1,0:T(8,128)(2,1)S(1)}, u32[]{:S(2)}, u32[]{:S(2)}) %all-to-all-start.1) | async-done | bytes 131104 | tf_op jit(solution)/shard_map/all_to_all | solution.py:77
  170.2 1.3 fusion.628
  171.8 2.1 fusion.391
  174.2 0.9 copy-done.2
  175.1 0.8 fusion.607
  176.0 0.7 all-gather.13.cloned.1.call-update
  176.7 0.8 fusion.612
  177.5 20.6 %all-gather.15.cloned.1.call-done = bf16[2048,1,16,32]{0,3,2,1:T(8,128)(2,1)} async-done(((bf16[256,1,16,32]{0,3,2,1:T(8,128)(2,1)}), bf16[2048,1,16,32]{0,3,2,1:T(8,128)(2,1)}) %all-gather.15.cloned.1.call-update) | async-done | bytes 2097168 | tf_op jit(solution)/shard_map/all_gather | solution.py:35
  198.1 17.1 %fusion.629 = (f32[16,256]{1,0:T(8,128)S(1)}, f32[16,256,2048]{2,1,0:T(8,128)}) fusion(bf16[2048,1,16,32]{0,3,2,1:T(8,128)(2,1)} %all-gather.15.cloned.1.call-done, bf16[256,3,16,32]{0,3,2,1:T(8,128)(2,1)} %copy-done.2), kind=kOutput, calls=%fused_computation.622 | convolution fusion | flops 562038784 | bytes 35930112 | tf_op jit(solution)/shard_map/sub | solution.py:26
  215.3 7.0 %all-gather.13.cloned.1.call-done = bf16[2048,1,16,32]{0,3,2,1:T(8,128)(2,1)} async-done(((bf16[256,1,16,32]{0,3,2,1:T(8,128)(2,1)}), bf16[2048,1,16,32]{0,3,2,1:T(8,128)(2,1)}) %all-gather.13.cloned.1.call-update) | async-done | bytes 2097168 | tf_op jit(solution)/shard_map/all_gather | solution.py:36
  222.3 18.0 %fusion.634 = (f32[256]{0:T(256)S(1)}, f32[256,512]{1,0:T(8,128)}) fusion(f32[512]{0:T(512)S(1)} %bitcast.393, f32[256,512]{1,0:T(8,128)} %copy-done.1, bf16[2,16,32,512]{3,2,1,0:T(8,128)(2,1)} %param.37, f32[16,256,2048]{2,1,0:T(8,128)} %get-tuple-element.74, f32[16,256]{1,0:T(8,128)S(1)} %get-tuple-element.73, ...), kind=kOutput, calls=%fused_computation.623 | convolution fusion | flops 688652032 | bytes 37243904 | tf_op jit(solution)/shard_map/nhe,hed->nd/dot_general | solution.py:38
  240.3 1.2 multiply_reduce_fusion.5
  241.6 8.9 %fusion.637 = (f32[256]{0:T(256)S(1)}, f32[256,512]{1,0:T(8,128)}) fusion(f32[512]{0:T(512)S(1)} %bitcast.390, f32[256,512]{1,0:T(8,128)} %get-tuple-element.76, bf16[2,2048,512]{2,1,0:T(8,128)(2,1)} %param.39, bf16[2,512,2048]{2,1,0:T(8,128)(2,1)} %param.38, f32[2048]{0:T(1024)S(1)} %bitcast.384, f32[512]{0:T(512)S(1)} %bitcast.391, ...), kind=kOutput, calls=%fused_computation.624 | convolution fusion | flops 1109655296 | bytes 5784576 | tf_op jit(solution)/shard_map/dot_general | solution.py:41
  250.5 1.2 multiply_reduce_fusion.4
  251.7 1.7 fusion.392
  253.8 0.8 fusion.606
  254.7 0.5 all-gather.17.cloned.1.call-update
  255.2 21.8 %all-gather.19.cloned.1.call-done = bf16[2048,1,16,32]{0,3,2,1:T(8,128)(2,1)} async-done(((bf16[256,1,16,32]{0,3,2,1:T(8,128)(2,1)}), bf16[2048,1,16,32]{0,3,2,1:T(8,128)(2,1)}) %all-gather.19.cloned.1.call-update) | async-done | bytes 2097168 | tf_op jit(solution)/shard_map/all_gather | solution.py:35
  277.0 17.2 %fusion.640 = (f32[16,256]{1,0:T(8,128)S(1)}, f32[16,256,2048]{2,1,0:T(8,128)}) fusion(bf16[2048,1,16,32]{0,3,2,1:T(8,128)(2,1)} %all-gather.19.cloned.1.call-done, bf16[256,3,16,32]{0,3,2,1:T(8,128)(2,1)S(1)} %add_convert_fusion), kind=kOutput, calls=%fused_computation.625 | convolution fusion | flops 562038784 | bytes 35930112 | tf_op jit(solution)/shard_map/sub | solution.py:26
  294.3 6.7 %all-gather.17.cloned.1.call-done = bf16[2048,1,16,32]{0,3,2,1:T(8,128)(2,1)} async-done(((bf16[256,1,16,32]{0,3,2,1:T(8,128)(2,1)}), bf16[2048,1,16,32]{0,3,2,1:T(8,128)(2,1)}) %all-gather.17.cloned.1.call-update) | async-done | bytes 2097168 | tf_op jit(solution)/shard_map/all_gather | solution.py:36
  301.0 14.9 %fusion.645 = (f32[256]{0:T(256)S(1)}, f32[256,512]{1,0:T(8,128)S(1)}) fusion(f32[512]{0:T(512)S(1)} %bitcast.389, f32[256,512]{1,0:T(8,128)S(1)} %copy-done.3, bf16[2,16,32,512]{3,2,1,0:T(8,128)(2,1)} %param.37, f32[16,256,2048]{2,1,0:T(8,128)} %get-tuple-element.80, f32[16,256]{1,0:T(8,128)S(1)} %get-tuple-element.79, ...), kind=kOutput, calls=%fused_computation.626 | convolution fusion | flops 688652032 | bytes 37243904 | tf_op jit(solution)/shard_map/nhe,hed->nd/dot_general | solution.py:38
  316.3 7.9 %fusion.648 = (f32[256]{0:T(256)S(1)}, f32[256,512]{1,0:T(8,128)S(1)}) fusion(f32[512]{0:T(512)S(1)} %bitcast.388, f32[256,512]{1,0:T(8,128)S(1)} %get-tuple-element.82, bf16[2,2048,512]{2,1,0:T(8,128)(2,1)} %param.39, bf16[2,512,2048]{2,1,0:T(8,128)(2,1)} %param.38, f32[2048]{0:T(1024)S(1)} %bitcast.383, f32[512]{0:T(512)S(1)} %bitcast.387, ...), kind=kOutput, calls=%fused_computation.627 | convolution fusion | flops 1109655296 | bytes 5784576 | tf_op jit(solution)/shard_map/dot_general | solution.py:41
  324.4 1.8 fusion.393
  (165 shorter events, 5.0 us)
Async XLA Ops:
  6.5 317.9 %copy-start = (bf16[512,1536]{1,0:T(8,128)(2,1)S(1)}, bf16[512,1536]{1,0:T(8,128)(2,1)}, u32[]{:S(2)}) copy-start(bf16[512,1536]{1,0:T(8,128)(2,1)} %param.41) | copy-start | bytes 4718596
  7.3 18.8 %copy-start.35 = (pred[256]{0:T(512)(128)(4,1)}, pred[256]{0:T(512)(128)(4,1)S(1)}, u32[]{:S(2)}) copy-start(pred[256]{0:T(512)(128)(4,1)S(1)} %broadcast_compare_fusion) | copy-start | bytes 772
  19.0 1.9 copy-start.50
  19.0 1.9 copy-start.52
  22.2 4.0 %copy-start.21 = (s32[256]{0:T(256)}, s32[256]{0:T(256)S(1)}, u32[]{:S(2)}) copy-start(s32[256]{0:T(256)S(1)} %add_bitcast_fusion) | copy-start | bytes 3076
  22.9 3.3 copy-start.6
  26.2 8.0 %copy-start.8 = (f32[2,12,512]{2,0,1:T(2,128)S(1)}, f32[2,12,512]{2,0,1:T(2,128)}, u32[]{:S(2)}) copy-start(f32[2,12,512]{2,0,1:T(2,128)} %param.35) | copy-start | bytes 147460
  26.5 6.3 %copy-start.7 = (f32[2,12,1280]{2,0,1:T(2,128)S(1)}, f32[2,12,1280]{2,0,1:T(2,128)}, u32[]{:S(2)}) copy-start(f32[2,12,1280]{2,0,1:T(2,128)} %param.27) | copy-start | bytes 368644
  29.3 15.1 %all-to-all-start = ((bf16[4,32,1280]{2,1,0:T(8,128)(2,1)}), bf16[4,32,1280]{2,1,0:T(8,128)(2,1)S(1)}, u32[]{:S(2)}, u32[]{:S(2)}) async-start(bf16[4,32,1280]{2,1,0:T(8,128)(2,1)} %bitcast.7), calls=%async_computation | async-start | bytes 655360 | tf_op jit(solution)/shard_map/all_to_all | solution.py:69
  35.4 3.4 %copy-start.51 = (s32[4,1]{0,1:T(1,128)S(1)}, s32[4,1]{0,1:T(1,128)}, u32[]{:S(2)}) copy-start(s32[4,1]{0,1:T(1,128)} %copy-done.50) | copy-start | bytes 52
  35.4 3.4 %copy-start.53 = (s32[4]{0:T(128)S(1)}, s32[4]{0:T(128)}, u32[]{:S(2)}) copy-start(s32[4]{0:T(128)} %copy-done.52) | copy-start | bytes 52
  35.4 4.0 %copy-start.23 = (f32[2,1280]{1,0:T(2,128)S(1)}, f32[2,1280]{1,0:T(2,128)}, u32[]{:S(2)}) copy-start(f32[2,1280]{1,0:T(2,128)} %param.32) | copy-start | bytes 30724
  35.4 4.9 %copy-start.27 = (f32[512]{0:T(512)S(1)}, f32[512]{0:T(512)}, u32[]{:S(2)}) copy-start(f32[512]{0:T(512)} %get-tuple-element.41) | copy-start | bytes 6148
  35.4 5.6 %copy-start.26 = (f32[512]{0:T(512)S(1)}, f32[512]{0:T(512)}, u32[]{:S(2)}) copy-start(f32[512]{0:T(512)} %get-tuple-element.42) | copy-start | bytes 6148
  35.4 6.3 %copy-start.25 = (f32[512]{0:T(512)S(1)}, f32[512]{0:T(512)}, u32[]{:S(2)}) copy-start(f32[512]{0:T(512)} %get-tuple-element.44) | copy-start | bytes 6148
  35.4 6.9 %copy-start.24 = (f32[512]{0:T(512)S(1)}, f32[512]{0:T(512)}, u32[]{:S(2)}) copy-start(f32[512]{0:T(512)} %get-tuple-element.43) | copy-start | bytes 6148
  43.1 0.5 copy-start.38
  69.8 17.6 %copy-start.34 = (f32[1280]{0:T(1024)S(1)}, f32[1280]{0:T(1024)}, u32[]{:S(2)}) copy-start(f32[1280]{0:T(1024)} %get-tuple-element.15) | copy-start | bytes 15364
  70.2 0.8 copy-start.4
  91.5 11.8 %copy-start.15 = (f32[3,16,80]{2,1,0:T(8,128)S(1)}, f32[3,16,80]{2,1,0:T(8,128)}, u32[]{:S(2)}) copy-start(f32[3,16,80]{2,1,0:T(8,128)} %get-tuple-element.61) | copy-start | bytes 46084
  91.6 11.8 %copy-start.32 = (f32[1280]{0:T(1024)S(1)}, f32[1280]{0:T(1024)}, u32[]{:S(2)}) copy-start(f32[1280]{0:T(1024)} %get-tuple-element.10) | copy-start | bytes 15364
  91.6 11.8 %copy-start.33 = (f32[1280]{0:T(1024)S(1)}, f32[1280]{0:T(1024)}, u32[]{:S(2)}) copy-start(f32[1280]{0:T(1024)} %get-tuple-element.11) | copy-start | bytes 15364
  111.2 32.9 %copy-start.31 = (f32[1280]{0:T(1024)S(1)}, f32[1280]{0:T(1024)}, u32[]{:S(2)}) copy-start(f32[1280]{0:T(1024)} %get-tuple-element.7) | copy-start | bytes 15364
  127.3 0.8 copy-start.5
  144.0 4.2 %copy-start.16 = (f32[1,4,1280]{2,0,1:T(1,128)S(1)}, f32[1,4,1280]{2,0,1:T(1,128)}, u32[]{:S(2)}) copy-start(f32[1,4,1280]{2,0,1:T(1,128)} %get-tuple-element.37) | copy-start | bytes 61444
  144.0 4.2 %copy-start.28 = (f32[1280]{0:T(1024)S(1)}, f32[1280]{0:T(1024)}, u32[]{:S(2)}) copy-start(f32[1280]{0:T(1024)} %get-tuple-element.5) | copy-start | bytes 15364
  144.1 4.2 %copy-start.29 = (f32[1280]{0:T(1024)S(1)}, f32[1280]{0:T(1024)}, u32[]{:S(2)}) copy-start(f32[1280]{0:T(1024)} %get-tuple-element.6) | copy-start | bytes 15364
  144.1 4.2 %copy-start.30 = (f32[1280]{0:T(1024)S(1)}, f32[1280]{0:T(1024)}, u32[]{:S(2)}) copy-start(f32[1280]{0:T(1024)} %get-tuple-element.20) | copy-start | bytes 15364
  148.3 11.8 %copy-start.9 = (f32[1280]{0:T(1024)S(1)}, f32[1280]{0:T(1024)}, u32[]{:S(2)}) copy-start(f32[1280]{0:T(1024)} %get-tuple-element.25) | copy-start | bytes 15364
  148.3 11.8 %copy-start.10 = (f32[1280]{0:T(1024)S(1)}, f32[1280]{0:T(1024)}, u32[]{:S(2)}) copy-start(f32[1280]{0:T(1024)} %get-tuple-element.26) | copy-start | bytes 15364
  148.3 13.5 %copy-start.40 = (pred[4,32]{1,0:T(4,128)(4,1)S(1)}, pred[4,32]{1,0:T(4,128)(4,1)}, u32[]{:S(2)}) copy-start(pred[4,32]{1,0:T(4,128)(4,1)} %compare_and_fusion) | copy-start | bytes 388
  159.8 6.7 %copy-start.11 = (f32[1,1,16,32]{3,2,1,0:T(8,128)S(1)}, f32[1,1,16,32]{3,2,1,0:T(8,128)}, u32[]{:S(2)}) copy-start(f32[1,1,16,32]{3,2,1,0:T(8,128)} %stack.39) | copy-start | bytes 6148
  159.8 6.7 %copy-start.12 = (f32[1,1,16,32]{3,2,1,0:T(8,128)S(1)}, f32[1,1,16,32]{3,2,1,0:T(8,128)}, u32[]{:S(2)}) copy-start(f32[1,1,16,32]{3,2,1,0:T(8,128)} %stack.41) | copy-start | bytes 6148
  159.8 6.7 %copy-start.13 = (f32[1,1,16,32]{3,2,1,0:T(8,128)S(1)}, f32[1,1,16,32]{3,2,1,0:T(8,128)}, u32[]{:S(2)}) copy-start(f32[1,1,16,32]{3,2,1,0:T(8,128)} %stack.43) | copy-start | bytes 6148
  159.8 6.7 %copy-start.14 = (f32[1,1,16,32]{3,2,1,0:T(8,128)S(1)}, f32[1,1,16,32]{3,2,1,0:T(8,128)}, u32[]{:S(2)}) copy-start(f32[1,1,16,32]{3,2,1,0:T(8,128)} %stack.44) | copy-start | bytes 6148
  159.8 6.7 %copy-start.39 = (f32[3]{0:T(128)S(1)}, f32[3]{0:T(128)}, u32[]{:S(2)}) copy-start(f32[3]{0:T(128)} %copy-done.38) | copy-start | bytes 40
  159.8 6.7 %copy-start.49 = (bf16[512]{0:T(512)(128)(2,1)S(1)}, bf16[512]{0:T(512)(128)(2,1)}, u32[]{:S(2)}) copy-start(bf16[512]{0:T(512)(128)(2,1)} %param.34) | copy-start | bytes 3076
  159.8 10.4 %copy-start.22 = (s32[256]{0:T(256)S(1)}, s32[256]{0:T(256)}, u32[]{:S(2)}) copy-start(s32[256]{0:T(256)} %copy-done.21) | copy-start | bytes 3076
  159.9 10.4 %copy-start.36 = (pred[256]{0:T(512)(128)(4,1)S(1)}, pred[256]{0:T(512)(128)(4,1)}, u32[]{:S(2)}) copy-start(pred[256]{0:T(512)(128)(4,1)} %copy-done.35) | copy-start | bytes 772
  159.9 11.9 %copy-start.19 = (f32[1,1,512]{2,0,1:T(1,128)S(1)}, f32[1,1,512]{2,0,1:T(1,128)}, u32[]{:S(2)}) copy-start(f32[1,1,512]{2,0,1:T(1,128)} %get-tuple-element.52) | copy-start | bytes 6148
  159.9 11.9 %copy-start.20 = (f32[1,1,512]{2,0,1:T(1,128)S(1)}, f32[1,1,512]{2,0,1:T(1,128)}, u32[]{:S(2)}) copy-start(f32[1,1,512]{2,0,1:T(1,128)} %get-tuple-element.53) | copy-start | bytes 6148
  162.5 7.7 %all-to-all-start.1 = ((bf16[4,32,512]{2,1,0:T(8,128)(2,1)}), bf16[4,32,512]{2,1,0:T(8,128)(2,1)S(1)}, u32[]{:S(2)}, u32[]{:S(2)}) async-start(bf16[4,32,512]{2,1,0:T(8,128)(2,1)} %broadcast_select_fusion), calls=%async_computation.1 | async-start | bytes 262144 | tf_op jit(solution)/shard_map/all_to_all | solution.py:77
  165.9 32.3 %all-gather.15.cloned.1.call-start = ((), (), s32[]{:S(2)}) async-start(), calls=%async_computation.3 | async-start | bytes 2359296 | tf_op jit(solution)/shard_map/all_gather | solution.py:35
  171.6 2.4 copy-start.1
  174.2 0.9 copy-start.2
  175.9 46.4 %all-gather.13.cloned.1.call-start = ((), (), s32[]{:S(2)}) async-start(), calls=%async_computation.2 | async-start | bytes 2359296 | tf_op jit(solution)/shard_map/all_gather | solution.py:36
  176.7 100.4 %all-gather.19.cloned.1.call-start = ((), (), s32[]{:S(2)}) async-start(), calls=%async_computation.5 | async-start | bytes 2359296 | tf_op jit(solution)/shard_map/all_gather | solution.py:35
  177.5 44.7 %copy-start.48 = (f32[1,1,512]{2,0,1:T(1,128)S(1)}, f32[1,1,512]{2,0,1:T(1,128)}, u32[]{:S(2)}) copy-start(f32[1,1,512]{2,0,1:T(1,128)} %get-tuple-element.50) | copy-start | bytes 6148
  222.3 19.3 %copy-start.45 = (f32[1,1,512]{2,0,1:T(1,128)S(1)}, f32[1,1,512]{2,0,1:T(1,128)}, u32[]{:S(2)}) copy-start(f32[1,1,512]{2,0,1:T(1,128)} %get-tuple-element.47) | copy-start | bytes 6148
  222.3 19.3 %copy-start.46 = (f32[1,1,512]{2,0,1:T(1,128)S(1)}, f32[1,1,512]{2,0,1:T(1,128)}, u32[]{:S(2)}) copy-start(f32[1,1,512]{2,0,1:T(1,128)} %get-tuple-element.48) | copy-start | bytes 6148
  222.3 19.3 %copy-start.47 = (f32[1,1,512]{2,0,1:T(1,128)S(1)}, f32[1,1,512]{2,0,1:T(1,128)}, u32[]{:S(2)}) copy-start(f32[1,1,512]{2,0,1:T(1,128)} %get-tuple-element.49) | copy-start | bytes 6148
  241.6 10.2 %copy-start.17 = (f32[1,1,512]{2,0,1:T(1,128)S(1)}, f32[1,1,512]{2,0,1:T(1,128)}, u32[]{:S(2)}) copy-start(f32[1,1,512]{2,0,1:T(1,128)} %get-tuple-element.45) | copy-start | bytes 6148
  241.6 10.2 %copy-start.18 = (f32[1,1,512]{2,0,1:T(1,128)S(1)}, f32[1,1,512]{2,0,1:T(1,128)}, u32[]{:S(2)}) copy-start(f32[1,1,512]{2,0,1:T(1,128)} %get-tuple-element.46) | copy-start | bytes 6148
  253.5 1.7 copy-start.37
  254.6 46.4 %all-gather.17.cloned.1.call-start = ((), (), s32[]{:S(2)}) async-start(), calls=%async_computation.4 | async-start | bytes 2359296 | tf_op jit(solution)/shard_map/all_gather | solution.py:36
  255.2 45.8 %copy-start.3 = (f32[256,512]{1,0:T(8,128)S(1)}, f32[256,512]{1,0:T(8,128)}, u32[]{:S(2)}) copy-start(f32[256,512]{1,0:T(8,128)} %get-tuple-element.78) | copy-start | bytes 1572868
  255.2 45.8 %copy-start.44 = (f32[1,1,512]{2,0,1:T(1,128)S(1)}, f32[1,1,512]{2,0,1:T(1,128)}, u32[]{:S(2)}) copy-start(f32[1,1,512]{2,0,1:T(1,128)} %get-tuple-element.51) | copy-start | bytes 6148
  301.0 15.2 %copy-start.41 = (f32[1,1,512]{2,0,1:T(1,128)S(1)}, f32[1,1,512]{2,0,1:T(1,128)}, u32[]{:S(2)}) copy-start(f32[1,1,512]{2,0,1:T(1,128)} %get-tuple-element.39) | copy-start | bytes 6148
  301.0 15.2 %copy-start.42 = (f32[1,1,512]{2,0,1:T(1,128)S(1)}, f32[1,1,512]{2,0,1:T(1,128)}, u32[]{:S(2)}) copy-start(f32[1,1,512]{2,0,1:T(1,128)} %get-tuple-element.40) | copy-start | bytes 6148
  301.0 15.2 %copy-start.43 = (f32[1,1,512]{2,0,1:T(1,128)S(1)}, f32[1,1,512]{2,0,1:T(1,128)}, u32[]{:S(2)}) copy-start(f32[1,1,512]{2,0,1:T(1,128)} %get-tuple-element.54) | copy-start | bytes 6148
Sparse Core Ops, SparseCore 0:
  176.0 22.0 all-gather.14
  200.0 22.2 all-gather.12
  254.7 22.2 all-gather.18
  278.7 22.2 all-gather.16
where the time goes:
time: 339 us; the launch traced here: 333 us
  matrix products  144 us (42%)
  blocking collectives  71.4 us (21%)
  waiting for transfers between devices  61.1 us (18%)
  local copies, waits for them, and re-layouts  21.7 us (6%)
  between operations  16.3 us (5%)
  other arithmetic  11.5 us (3%)
  starting transfers between devices  7.46 us (2%)
    all_gather x2, waiting for transfers between devices, run_block(): key_rows = gather_rows(qkv_rows[:, 1])  42.4 us
    dot_general x4, matrix products, run_block(): jnp.einsum('nhe,hed->nd', attended, w_o, preferred_element_type=jnp.float32)  40.8 us
    dot_general x4, matrix products, run_block(): jnp.dot(mlp_hidden, w_two, preferred_element_type=jnp.float32)  39.8 us
    sub x2, matrix products, attend(): attn_probs = jax.nn.softmax(scores, axis=-1).astype(jnp.bfloat16)  34.4 us
    all_gather x2, blocking collectives, run_block(): key_rows = gather_rows(qkv_rows[:, 1])  32.9 us
    all_gather x2, blocking collectives, run_block(): value_rows = gather_rows(qkv_rows[:, 2])  31.7 us
    dot_general x2, matrix products, run_block(): jnp.einsum('nd,dche->nche', normed, w_qkv, preferred_element_type=jnp.flo...  15.5 us
    all_gather x2, waiting for transfers between devices, run_block(): value_rows = gather_rows(qkv_rows[:, 2])  13.7 us
  transfers between devices with their start and end apart: 6, of which 5 were waited for; matrix products, arithmetic and copies ran while one was open for 14% of the time, Pallas kernels for 0%

commit v1 on v0

v1 whole, which is shorter than its diff:
```python
import functools
import math

import jax
import jax.numpy as jnp
from jax import lax
from jax.experimental import pallas as pl
from jax.experimental.pallas import tpu as pltpu
from jax.sharding import PartitionSpec as P

LN_EPS = 1e-6
MESH = pl.DeviceIdType.MESH
TOKEN_AXES = ("batch", "time", "region")
F32, BF16 = jnp.float32, jnp.bfloat16
NT = (((1,), (1,)), ((), ()))
TN = (((0,), (0,)), ((), ()))
NN = (((1,), (0,)), ((), ()))
LOG2E = 1.4426950408889634
BIG, MID = 66_000_000, 60_000_000
LANES, TOK, ENC, DEC = 128, 256, 1280, 512
PART, HID, CODED, KEYS, ALL = 640, 2560, 640, 2048, 1536


def vm(*shape):
    return pltpu.VMEM(shape, BF16)


def vmf(*shape):
    return pltpu.VMEM(shape, F32)


def mm(lhs, rhs, dims=NN):
    return lax.dot_general(lhs, rhs, dims, preferred_element_type=F32)


def norm(x, gain, shift):
    mean = jnp.mean(x, axis=-1, keepdims=True)
    cen = x - mean
    var = jnp.mean(cen * cen, axis=-1, keepdims=True)
    return cen * lax.rsqrt(var + LN_EPS) * gain + shift


def norm_rows(src, dst, gain, shift, step):
    def body(i, _):
        rows = pl.ds(pl.multiple_of(i * step, step), step)
        dst[rows, :] = norm(src[rows, :].astype(F32), gain, shift).astype(BF16)
        return 0
    lax.fori_loop(0, src.shape[0] // step, body, 0)


def gelu(x):
    return 0.5 * x * (1.0 + lax.erf(x * (0.5 ** 0.5)))


def column(row, lanes):
    wide = jnp.broadcast_to(row, (LANES, row.shape[1])).T
    return jnp.concatenate([wide] * (lanes // LANES), axis=1)


def neighbours():
    time, region = lax.axis_index("time"), lax.axis_index("region")
    mate = {"batch": 0, "time": time, "region": region + 1 - 2 * (region % 2)}
    across = {"batch": 0, "time": time, "region": (region + 2) % 4}
    along = {"batch": 0, "time": 1 - time, "region": region}
    return mate, across, along


def greet(peers):
    barrier = pltpu.get_barrier_semaphore()
    for peer in peers:
        pl.semaphore_signal(barrier, inc=1, device_id=peer, device_id_type=MESH)
    pl.semaphore_wait(barrier, len(peers))


def push(src, dst, send, recv, peer):
    return pltpu.make_async_remote_copy(src_ref=src, dst_ref=dst, send_sem=send, recv_sem=recv, device_id=peer, device_id_type=MESH)


class Gather:
    def __init__(self, src, slots, send, recv):
        self.mate, self.across, self.along = neighbours()
        half = slots.shape[1] // 2
        top, low = pl.ds(0, half), pl.ds(half, half)
        c = lambda i, s, d, peer: push(s, d, send.at[i], recv.at[i], peer)
        self.first = [c(0, src, slots.at[1], self.mate), c(1, src, slots.at[2], self.across), c(2, src, slots.at[4], self.along)]
        self.from_x = [c(3, slots.at[2, top], slots.at[6, top], self.along), c(4, slots.at[2], slots.at[3], self.mate)]
        self.from_y = [c(5, slots.at[4, low], slots.at[6, low], self.across), c(6, slots.at[4], slots.at[5], self.mate)]
        self.last = [c(7, slots.at[6, top], slots.at[7, top], self.mate), c(8, slots.at[6, low], slots.at[7, low], self.mate)]

    def start(self):
        for copy in self.first:
            copy.start()

    def relay(self):
        self.first[1].wait_recv()
        for copy in self.from_x:
            copy.start()
        self.first[2].wait_recv()
        for copy in self.from_y:
            copy.start()

    def relay_last(self):
        self.from_x[0].wait_recv()
        self.last[0].start()
        self.from_y[0].wait_recv()
        self.last[1].start()

    def finish(self):
        for copy in (self.first[0], self.from_x[1], self.from_y[1], *self.last):
            copy.wait_recv()

    def drain(self):
        for copy in (*self.first, *self.from_x, *self.from_y, *self.last):
            copy.wait_send()


def encoder_kernel(patches, enc_pos, mask, dec_pos, b_embed, vec, fin, w_embed, w_qkv, w_o, w_one, w_two, w_dec,
                   z_out, dall,
                   wemb, wqkv, wo, w1, w2, wdec, ebuf, drecv, csum, xrecv, hb, h, a, qkv, att, g, xs, xr, dsrc,
                   wsem, esend, erecv, xsend, xrecvs, gsend, grecv, osem):
    layers = w_qkv.shape[0]
    core = lax.axis_index("region") % 2
    mate, across, along = neighbours()
    width = h.shape[1]
    heads = 8
    dim = qkv.shape[1] // heads
    part = qkv.shape[1]
    hid = w1.shape[2]
    feats = pl.ds(pl.multiple_of(core * part, LANES), part)
    hids = pl.ds(pl.multiple_of(core * hid, LANES), hid)

    load_embed = pltpu.make_async_copy(w_embed, wemb, wsem.at[0])
    load_embed.start()
    greet([mate, across, along])

    mrow = mask[:].astype(F32).astype(BF16)
    tok = mrow.shape[1]
    row_id = lax.broadcasted_iota(jnp.int32, (tok, tok), 0)
    col_id = lax.broadcasted_iota(jnp.int32, (tok, tok), 1)
    upper = (row_id <= col_id).astype(F32).astype(BF16)
    lower = (row_id >= col_id).astype(F32).astype(BF16)
    same = (row_id == col_id).astype(F32).astype(BF16)
    mrows = jnp.broadcast_to(mrow, (LANES, tok))
    rank = mm(mrows, upper)
    slot = lax.broadcasted_iota(jnp.int32, (LANES, tok), 0).astype(F32) + 1.0
    sel_f = jnp.where((rank == slot) & (mrows.astype(F32) > 0.5), 1.0, 0.0)
    sel = sel_f.astype(BF16)
    valid = jnp.sum(sel_f, axis=1, keepdims=True) > 0.5
    code = mm(lower, mrows, NT) * mm(same, mrows, NT)
    dsrc[:, 0:DEC] = dec_pos[:]
    dsrc[:, DEC:PART] = code.astype(BF16)
    picked = mm(sel, patches[:]).astype(BF16)

    load_embed.wait()
    loads = {}
    k = 1
    for l in range(layers):
        for w in range(3):
            loads["qkv", l, w] = pltpu.make_async_copy(w_qkv.at[l, w, feats], wqkv.at[l, w], wsem.at[k + w])
        loads["o", l] = pltpu.make_async_copy(w_o.at[l, feats], wo.at[l], wsem.at[k + 3])
        loads["one", l] = pltpu.make_async_copy(w_one.at[l, :, hids], w1.at[l], wsem.at[k + 4])
        loads["two", l] = pltpu.make_async_copy(w_two.at[l, hids], w2.at[l], wsem.at[k + 5])
        k += 6
    loads["dec"] = pltpu.make_async_copy(w_dec, wdec, wsem.at[k])
    for load in loads.values():
        load.start()

    chunks = width // TOK
    pairs, xs1, ys1, f1, f2 = [], [], [], [], []
    for j in range(chunks):
        pairs.append(push(ebuf.at[j, 1 - core], drecv.at[j], esend.at[0, j], erecv.at[0, j], mate))
        xs1.append(push(csum.at[j], xrecv.at[j], esend.at[1, j], erecv.at[1, j], across))
        ys1.append(push(hb.at[0, core, j], hb.at[1, core, j], esend.at[2, j], erecv.at[2, j], along))
        f1.append(push(hb.at[0, core, j], hb.at[0, core, j], esend.at[3, j], erecv.at[3, j], mate))
        f2.append(push(hb.at[1, core, j], hb.at[1, core, j], esend.at[4, j], erecv.at[4, j], mate))
    for j in range(chunks):
        cols = slice(TOK * j, TOK * (j + 1))
        e = mm(picked, wemb[:, cols]) + b_embed[:, cols] + mm(sel, enc_pos[:, cols])
        e = jnp.where(valid, e, 0.0).astype(BF16)
        ebuf[j, 0] = e[:, :LANES]
        ebuf[j, 1] = e[:, LANES:]
        pairs[j].start()
    for j in range(chunks):
        pairs[j].wait_recv()
        csum[j] = ebuf[j, core] + drecv[j]
        xs1[j].start()
    for j in range(chunks):
        xs1[j].wait_recv()
        hb[0, core, j] = csum[j] + xrecv[j]
        ys1[j].start()
        f1[j].start()
    for j in range(chunks):
        ys1[j].wait_recv()
        f2[j].start()
    in_f1 = [push(hb.at[0, 1 - core, j], hb.at[0, 1 - core, j], esend.at[3, j], erecv.at[3, j], mate) for j in range(chunks)]
    in_f2 = [push(hb.at[1, 1 - core, j], hb.at[1, 1 - core, j], esend.at[4, j], erecv.at[4, j], mate) for j in range(chunks)]
    for j in range(chunks):
        in_f1[j].wait_recv()
        in_f2[j].wait_recv()
    for j in range(chunks):
        for copy in (pairs[j], xs1[j], ys1[j], f1[j], f2[j]):
            copy.wait_send()

    gather = Gather(dsrc, dall, gsend, grecv)
    own = pltpu.make_async_copy(dsrc, dall.at[0], osem.at[0])
    own.start()
    gather.start()

    for t in range(2):
        for half in range(2):
            for j in range(chunks):
                h[LANES * t:LANES * (t + 1), TOK * j + LANES * half:TOK * j + LANES * half + LANES] = hb[t, half, j]

    def exchange(slot):
        return [push(xs.at[slot, j], xr.at[slot, j], xsend.at[slot, j], xrecvs.at[slot, j], mate) for j in range(chunks)]

    for l in range(layers):
        norm_rows(h, a, vec[0, l:l + 1, :], vec[1, l:l + 1, :], 64)
        for w in range(3):
            loads["qkv", l, w].wait()
            r = mm(wqkv[l, w], a[:], NT)
            if w != 1:
                r = r + column(vec[4 if w == 0 else 5, l:l + 1, feats], TOK)
            qkv[w] = r.astype(BF16)
        for hd in range(heads):
            rows = slice(hd * dim, (hd + 1) * dim)
            s = mm(qkv[1, rows], qkv[0, rows], TN) * (dim ** -0.5)
            p = jnp.exp(s - jnp.max(s, axis=0, keepdims=True))
            p = p * (1.0 / jnp.sum(p, axis=0, keepdims=True))
            att[rows, :] = mm(qkv[2, rows], p.astype(BF16)).astype(BF16)
        loads["o", l].wait()
        copies = exchange(0)
        for j in range(chunks):
            if l > 0:
                copies[j].wait_send()
            xs[0, j] = mm(att[:], wo[l, :, TOK * j:TOK * (j + 1)], TN)
            copies[j].start()
        if l == 0:
            gather.relay()
        else:
            gather.relay_last()
        for j in range(chunks):
            cols = slice(TOK * j, TOK * (j + 1))
            copies[j].wait_recv()
            h[:, cols] = (h[:, cols].astype(F32) + (xs[0, j] + xr[0, j]) + vec[6, l:l + 1, cols]).astype(BF16)
        norm_rows(h, a, vec[2, l:l + 1, :], vec[3, l:l + 1, :], 64)
        loads["one", l].wait()
        for j in range(hid // TOK):
            cols = slice(TOK * j, TOK * (j + 1))
            at = (TOK * j) % width
            bias = vec[8 + (hid // width) * core + (TOK * j) // width, l:l + 1, at:at + TOK]
            g[:, cols] = gelu(mm(a[:], w1[l, :, cols]) + bias).astype(BF16)
        loads["two", l].wait()
        copies = exchange(1)
        for j in range(chunks):
            if l > 0:
                copies[j].wait_send()
            xs[1, j] = mm(g[:], w2[l, :, TOK * j:TOK * (j + 1)])
            copies[j].start()
        for j in range(chunks):
            cols = slice(TOK * j, TOK * (j + 1))
            copies[j].wait_recv()
            h[:, cols] = (h[:, cols].astype(F32) + (xs[1, j] + xr[1, j]) + vec[7, l:l + 1, cols]).astype(BF16)
    norm_rows(h, a, fin[0:1, :], fin[1:2, :], 64)
    loads["dec"].wait()
    z_out[:] = mm(a[:], wdec[:]).astype(BF16)
    for slot in range(2):
        for copy in exchange(slot):
            copy.wait_send()
    gather.finish()
    gather.drain()
    own.wait()


def attend(q, kt, vt, att, buf, peak, heads, dim, keys):
    scale = dim ** -0.5 * LOG2E
    tiles = keys // TOK

    def rows_of(hd):
        return pl.ds(pl.multiple_of(hd * dim, dim), dim)

    def step(score_hd, score_slot, hd, slot):
        best = jnp.full((8, TOK), -jnp.inf, F32)
        if hd is not None:
            top = jnp.max(peak[slot], axis=0, keepdims=True) * scale
            total = jnp.zeros((8, TOK), F32)
            out = jnp.zeros((dim, TOK), F32)
        for i in range(tiles):
            cols = slice(TOK * i, TOK * (i + 1))
            s = mm(kt[rows_of(score_hd), cols], q[rows_of(score_hd), :], TN)
            buf[score_slot][cols, :] = s
            best = jnp.maximum(best, jnp.max(s.reshape(32, 8, TOK), axis=0))
            if hd is not None:
                p = jnp.exp2(buf[slot][cols, :] * scale - top)
                total = total + jnp.sum(p.reshape(32, 8, TOK), axis=0)
                out = out + mm(vt[rows_of(hd), cols], p.astype(BF16))
        peak[score_slot] = best
        if hd is not None:
            total = jnp.sum(total, axis=0, keepdims=True)
            att[rows_of(hd), :] = (out * (1.0 / total)).astype(BF16)

    step(0, 0, None, None)

    def body(i, _):
        step(2 * i + 1, 1, 2 * i, 0)
        step(jnp.minimum(2 * i + 2, heads - 1), 0, 2 * i + 1, 1)
        return 0
    lax.fori_loop(0, heads // 2, body, 0)


def block_tail(h, att, a, g, vec, l, wo, w1, w2):
    h[:] = (h[:].astype(F32) + mm(att[:], wo[:], TN) + vec[6, l:l + 1, :]).astype(BF16)
    norm_rows(h, a, vec[2, l:l + 1, :], vec[3, l:l + 1, :], LANES)
    width = h.shape[1]
    for j in range(w1.shape[1] // width):
        cols = slice(width * j, width * (j + 1))
        g[:, cols] = gelu(mm(a[:], w1[:, cols]) + vec[8 + j, l:l + 1, :]).astype(BF16)
    h[:] = (h[:].astype(F32) + mm(g[:], w2[:]) + vec[7, l:l + 1, :]).astype(BF16)


def decoder_loads(l, w_qkv, w_o, w_one, w_two, wqkv, wo, w1, w2, wsem):
    pairs = ((w_qkv, wqkv), (w_o, wo), (w_one, w1), (w_two, w2))
    return [pltpu.make_async_copy(src.at[l], dst, wsem.at[i]) for i, (src, dst) in enumerate(pairs)]


def keys_values(rows, a_rows, cols, wqkv, kt, vt, vbias):
    kt[:, cols] = mm(wqkv[rows:2 * rows, :], a_rows, NT).astype(BF16)
    vt[:, cols] = (mm(wqkv[2 * rows:, :], a_rows, NT) + vbias[:]).astype(BF16)


def first_decoder_kernel(z, dall, token, vec, w_qkv, w_o, w_one, w_two, h_out, a_out,
                         wqkv, wo, w1, w2, h, a, kt, vt, q, att, g, buf0, buf1, peak, vbias, wsem):
    width = h.shape[1]
    loads = decoder_loads(0, w_qkv, w_o, w_one, w_two, wqkv, wo, w1, w2, wsem)
    for load in loads:
        load.start()
    vbias[:] = column(vec[5, 0:1, :], TOK)
    lane = lax.broadcasted_iota(jnp.int32, (TOK, LANES), 1).astype(F32) + 1.0
    loads[0].wait()

    def build(i, _):
        code = dall[i, :, DEC:PART].astype(F32)
        pick = jnp.where(code == lane, 1.0, 0.0).astype(BF16)
        block = jnp.where(i < 4, 0, LANES)
        placed = mm(pick, z[pl.ds(pl.multiple_of(block, LANES), LANES), :])
        seen = code[:, 0:1] > 0.5
        u = (jnp.where(seen, placed, token[:].astype(F32)) + dall[i, :, 0:DEC].astype(F32)).astype(BF16)
        a_rows = norm(u.astype(F32), vec[0, 0:1, :], vec[1, 0:1, :]).astype(BF16)

        @pl.when(i == 0)
        def _():
            h[:] = u
            a[:] = a_rows
        keys_values(width, a_rows, pl.ds(pl.multiple_of(i * TOK, TOK), TOK), wqkv, kt, vt, vbias)
        return 0
    lax.fori_loop(0, 8, build, 0)
    q[:] = (mm(wqkv[0:width, :], a[:], NT) + column(vec[4, 0:1, :], TOK)).astype(BF16)
    attend(q, kt, vt, att, (buf0, buf1), peak, 16, width // 16, KEYS)
    for load in loads[1:]:
        load.wait()
    block_tail(h, att, a, g, vec, 0, wo, w1, w2)
    h_out[:] = h[:]
    norm_rows(h, a_out, vec[0, 1:2, :], vec[1, 1:2, :], LANES)


def last_decoder_kernel(h_in, a_in, vec, fin, w_qkv, w_o, w_one, w_two, y_out,
                        wqkv, wo, w1, w2, h, a, aall, kt, vt, q, att, g, buf0, buf1, peak, vbias, wsem, gsend, grecv):
    width = h.shape[1]
    loads = decoder_loads(1, w_qkv, w_o, w_one, w_two, wqkv, wo, w1, w2, wsem)
    greet(neighbours())
    gather = Gather(a_in, aall, gsend, grecv)
    gather.start()
    for load in loads:
        load.start()
    h[:] = h_in[:]
    vbias[:] = column(vec[5, 1:2, :], TOK)
    loads[0].wait()
    q[:] = (mm(wqkv[0:width, :], a_in[:], NT) + column(vec[4, 1:2, :], TOK)).astype(BF16)
    keys_values(width, a_in[:], slice(0, TOK), wqkv, kt, vt, vbias)
    gather.relay()
    gather.relay_last()
    gather.finish()

    def build(i, _):
        keys_values(width, aall[i], pl.ds(pl.multiple_of(i * TOK, TOK), TOK), wqkv, kt, vt, vbias)
        return 0
    lax.fori_loop(1, 8, build, 0)
    attend(q, kt, vt, att, (buf0, buf1), peak, 16, width // 16, KEYS)
    for load in loads[1:]:
        load.wait()
    block_tail(h, att, a, g, vec, 1, wo, w1, w2)
    norm_rows(h, y_out, fin[0:1, :], fin[1:2, :], LANES)
    gather.drain()


VM = pl.BlockSpec(memory_space=pltpu.VMEM)
HB = pl.BlockSpec(memory_space=pl.ANY)


def decoder_scratch():
    return [
        vm(ALL, DEC), vm(DEC, DEC), vm(DEC, KEYS), vm(KEYS, DEC),
        vm(TOK, DEC), vm(TOK, DEC),
    ], [
        vm(DEC, KEYS), vm(DEC, KEYS), vm(DEC, TOK), vm(DEC, TOK),
        vm(TOK, KEYS), vmf(KEYS, TOK), vmf(KEYS, TOK), vmf(2, 8, TOK),
        vmf(DEC, TOK), pltpu.SemaphoreType.DMA((4,)),
    ]


def solution(mesh):
    def local_step(patches, enc_pos, vis_mask, dec_pos, w_embed, b_embed, enc_vec, enc_wqkv, enc_wo, enc_w1, enc_w2, enc_final, w_dec_in, mask_token, dec_vec, dec_wqkv, dec_wo, dec_w1, dec_w2, dec_final, w_out):
        layers = enc_vec.shape[0]
        evec = jnp.transpose(enc_vec, (1, 0, 2))
        dvec = jnp.transpose(dec_vec, (1, 0, 2))
        ewqkv = jnp.transpose(enc_wqkv, (0, 2, 3, 4, 1)).reshape(layers, 3, ENC, ENC)
        ewo = enc_wo.reshape(layers, ENC, ENC)
        dwqkv = jnp.transpose(dec_wqkv, (0, 2, 3, 4, 1)).reshape(layers, ALL, DEC)
        dwo = dec_wo.reshape(layers, DEC, DEC)
        dma = pltpu.SemaphoreType.DMA
        z, dall = pl.pallas_call(
            encoder_kernel,
            out_shape=(jax.ShapeDtypeStruct((TOK, DEC), BF16), jax.ShapeDtypeStruct((8, TOK, PART), BF16)),
            in_specs=[VM] * 7 + [HB] * 6,
            out_specs=(VM, HB),
            scratch_shapes=[
                vm(ALL, ENC),
                vm(layers, 3, PART, ENC), vm(layers, PART, ENC),
                vm(layers, ENC, HID), vm(layers, HID, ENC), vm(ENC, DEC),
                vm(5, 2, LANES, LANES), vm(5, LANES, LANES), vm(5, LANES, LANES),
                vm(5, LANES, LANES), vm(2, 2, 5, LANES, LANES),
                vm(TOK, ENC), vm(TOK, ENC),
                vm(3, PART, TOK), vm(PART, TOK), vm(TOK, HID),
                vmf(2, 5, TOK, TOK), vmf(2, 5, TOK, TOK), vm(TOK, PART),
                dma((14,)), dma((5, 5)), dma((5, 5)), dma((2, 5)), dma((2, 5)), dma((9,)), dma((9,)), dma((1,)),
            ],
            compiler_params=pltpu.CompilerParams(collective_id=0, has_side_effects=True, vmem_limit_bytes=BIG),
            name="encoder",
        )(patches, enc_pos, vis_mask.reshape(1, -1), dec_pos, b_embed.reshape(1, -1), evec, enc_final, w_embed, ewqkv, ewo, enc_w1, enc_w2, w_dec_in)
        head, tail = decoder_scratch()
        rows = jax.ShapeDtypeStruct((TOK, DEC), BF16)
        h, a = pl.pallas_call(
            first_decoder_kernel,
            out_shape=(rows, rows),
            in_specs=[VM] * 4 + [HB] * 4,
            out_specs=(VM, VM),
            scratch_shapes=head + tail,
            compiler_params=pltpu.CompilerParams(vmem_limit_bytes=MID),
            name="decoder_first",
        )(z, dall, mask_token.reshape(1, -1), dvec, dwqkv, dwo, dec_w1, dec_w2)
        y = pl.pallas_call(
            last_decoder_kernel,
            out_shape=rows,
            in_specs=[VM] * 4 + [HB] * 4,
            out_specs=VM,
            scratch_shapes=head + [vm(8, TOK, DEC)] + tail + [dma((9,)), dma((9,))],
            compiler_params=pltpu.CompilerParams(collective_id=1, has_side_effects=True, vmem_limit_bytes=MID),
            name="decoder_last",
        )(h, a, dvec, dec_final, dwqkv, dwo, dec_w1, dec_w2)
        return jnp.dot(y, w_out, preferred_element_type=F32)

    token_rows = P(TOKEN_AXES, None)
    in_specs = (token_rows, token_rows, P(TOKEN_AXES), token_rows) + (P(),) * 17
    return jax.shard_map(local_step, mesh=mesh, in_specs=in_specs, out_specs=token_rows, check_vma=False)
```

time: 339 us -> 120 us (0.35); the launches traced: 333 us -> 119 us
  matrix products: 144 us -> 2.67 us
  Pallas kernels: 0 us -> 114 us
  blocking collectives: 71.4 us -> 0 us
  waiting for transfers between devices: 61.1 us -> 0 us
  local copies, waits for them, and re-layouts: 21.7 us -> 2.57 us
  between operations: 16.3 us -> 0.04 us
  other arithmetic: 11.5 us -> 0 us
  starting transfers between devices: 7.46 us -> 0 us
    pallas_call x0 -> x3, Pallas kernels: none -> 114 us  [the longest x1 56.3 us: local_step(): pl.pallas_call(encoder_kernel, out_shape=(jax.ShapeDtypeStruct((TOK, DEC)...]
    dot_general x17 -> x1, matrix products: 105 us -> 2.67 us  [local_step(): return jnp.dot(y, w_out, preferred_element_type=F32)]
    all_gather x4 -> x0, blocking collectives: 64.6 us -> none  [the longest x2 32.9 us: run_block(): key_rows = gather_rows(qkv_rows[:, 1])]
    all_gather x4 -> x0, waiting for transfers between devices: 56.2 us -> none  [the longest x2 42.4 us: run_block(): key_rows = gather_rows(qkv_rows[:, 1])]
    sub x2 -> x0, matrix products: 34.4 us -> none  [attend(): attn_probs = jax.nn.softmax(scores, axis=-1).astype(jnp.bfloat16)]
    slice x13 -> x0, local copies, waits for them, and re-layouts: 9.93 us -> none  [the longest x1 3.35 us: local_step(): dec_wqkv[layer_idx]]
    all_to_all x2 -> x0, starting transfers between devices: 6.78 us -> none  [the longest x1 3.45 us: local_step(): received = lax.all_to_all(send_rows, 'region', 0, 0, tiled=True)]
    unnamed x1 -> x0, blocking collectives: 6.75 us -> none
  transfers between devices with their start and end apart: 6 -> 0, of which waited for: 5 -> 0; matrix products, arithmetic and copies ran while one was open for 14% -> 0% of each run, Pallas kernels for 0% -> 0%
where the time goes in v1:
time: 120 us; the launch traced here: 119 us
  Pallas kernels  114 us (95%)
  matrix products  2.67 us (2%)
  local copies, waits for them, and re-layouts  2.57 us (2%)
    pallas_call x1, Pallas kernels, local_step(): pl.pallas_call(encoder_kernel, out_shape=(jax.ShapeDtypeStruct((TOK, DEC)...  56.3 us
    pallas_call x1, Pallas kernels, local_step(): pl.pallas_call(last_decoder_kernel, out_shape=rows, in_specs=[VM] * 4 + [...  32.2 us
    pallas_call x1, Pallas kernels, local_step(): pl.pallas_call(first_decoder_kernel, out_shape=(rows, rows), in_specs=[VM...  25.4 us
    dot_general x1, matrix products, local_step(): return jnp.dot(y, w_out, preferred_element_type=F32)  2.67 us

profile of v1, /device:TPU:0, one launch (start us, length us, event | category | flops | bytes accessed | tf_op | source)
XLA Modules:
  0.0 119.2 jit_solution(3558583620001703454)
XLA Ops:
  0.0 1.3 %reshape.25.token = bf16[1,512]{1,0:T(2,128)(2,1)} reshape(bf16[512]{0:T(512)(128)(2,1)} %param.34) | data formatting | bytes 2048 | tf_op jit(solution)/shard_map/reshape | solution.py:450
  1.3 1.3 %reshape.22.b_embed = f32[1,1280]{1,0:T(1,128)} reshape(f32[1280]{0:T(1024)} %param.26) | data formatting | bytes 10240 | tf_op jit(solution)/shard_map/reshape | solution.py:439
  2.6 56.3 %encoder.1 = (bf16[256,512]{1,0:T(8,128)(2,1)}, bf16[8,256,640]{2,1,0:T(8,128)(2,1)}) custom-call(bf16[256,1536]{1,0:T(8,128)(2,1)} %patches.1, bf16[256,1280]{1,0:T(8,128)(2,1)} %enc_pos.1, s32[1,256]{1,0:T(1,128)} %bitcast.22, bf16[256,512]{1,0:T(8,128)(2,1)} %dec_pos.1, f32[1,1280]{1,0:T(1,128)} %reshape.22.b_embed, f32[12,2,1280]{2,1,0:T(2,128)} %bitcast.21, ...), custom_call_target="tpu_custom_call" | custom-call | tf_op jit(solution)/shard_map/encoder/pallas_call | solution.py:421
  58.9 25.4 %decoder_first.1 = (bf16[256,512]{1,0:T(8,128)(2,1)}, bf16[256,512]{1,0:T(8,128)(2,1)}) custom-call(bf16[256,512]{1,0:T(8,128)(2,1)} %get-tuple-element.9.z, bf16[8,256,640]{2,1,0:T(8,128)(2,1)} %get-tuple-element.10.dall, bf16[1,512]{1,0:T(2,128)(2,1)} %reshape.25.token, f32[12,2,512]{2,1,0:T(2,128)} %bitcast.19, bf16[2,1536,512]{2,1,0:T(8,128)(2,1)} %bitcast.14, ...), custom_call_target="tpu_custom_call" | custom-call | tf_op jit(solution)/shard_map/decoder_first/pallas_call | solution.py:442
  84.3 0.0 copy-start
  84.3 32.2 %decoder_last.1 = bf16[256,512]{1,0:T(8,128)(2,1)} custom-call(bf16[256,512]{1,0:T(8,128)(2,1)} %get-tuple-element.11.h_in, bf16[256,512]{1,0:T(8,128)(2,1)} %get-tuple-element.12.a_in, f32[12,2,512]{2,1,0:T(2,128)} %bitcast.20, f32[2,512]{1,0:T(2,128)} %fin.3, bf16[2,1536,512]{2,1,0:T(8,128)(2,1)} %bitcast.15, bf16[2,512,512]{2,1,0:T(8,128)(2,1)} %bitcast.18, ...), custom_call_target="tpu_custom_call" | custom-call | tf_op jit(solution)/shard_map/decoder_last/pallas_call | solution.py:451
  116.5 0.0 copy-done
  116.5 2.7 %fusion = f32[256,1536]{1,0:T(8,128)} fusion(bf16[256,512]{1,0:T(8,128)(2,1)} %decoder_last.1, bf16[512,1536]{1,0:T(8,128)(2,1)S(1)} %copy-done), kind=kOutput, calls=%fused_computation | convolution fusion | flops 402653184 | bytes 3407872 | tf_op jit(solution)/shard_map/dot_general | solution.py:460
Async XLA Ops:
  84.3 32.2 %copy-start = (bf16[512,1536]{1,0:T(8,128)(2,1)S(1)}, bf16[512,1536]{1,0:T(8,128)(2,1)}, u32[]{:S(2)}) copy-start(bf16[512,1536]{1,0:T(8,128)(2,1)} %param.41) | copy-start | bytes 4718596

commit v2 on v1

v2 whole, which is shorter than its diff:
```python
import functools
import math

import jax
import jax.numpy as jnp
from jax import lax
from jax.experimental import pallas as pl
from jax.experimental.pallas import tpu as pltpu
from jax.sharding import PartitionSpec as P

LN_EPS = 1e-6
MESH = pl.DeviceIdType.MESH
TOKEN_AXES = ("batch", "time", "region")
F32, BF16 = jnp.float32, jnp.bfloat16
NT = (((1,), (1,)), ((), ()))
TN = (((0,), (0,)), ((), ()))
NN = (((1,), (0,)), ((), ()))
LOG2E = 1.4426950408889634
BIG, MID = 66_000_000, 60_000_000
LANES, TOK, ENC, DEC = 128, 256, 1280, 512
PART, HID, CODED, KEYS, ALL = 640, 2560, 640, 2048, 1536


def vm(*shape):
    return pltpu.VMEM(shape, BF16)


def vmf(*shape):
    return pltpu.VMEM(shape, F32)


def mm(lhs, rhs, dims=NN):
    return lax.dot_general(lhs, rhs, dims, preferred_element_type=F32)


def norm(x, gain, shift):
    mean = jnp.mean(x, axis=-1, keepdims=True)
    cen = x - mean
    var = jnp.mean(cen * cen, axis=-1, keepdims=True)
    return cen * lax.rsqrt(var + LN_EPS) * gain + shift


def norm_rows(src, dst, gain, shift, step):
    for i in range(src.shape[0] // step):
        rows = slice(i * step, (i + 1) * step)
        dst[rows, :] = norm(src[rows, :].astype(F32), gain, shift).astype(BF16)


def gelu(x):
    return 0.5 * x * (1.0 + lax.erf(x * (0.5 ** 0.5)))


def column(row):
    return jnp.broadcast_to(row, (LANES, row.shape[1])).T


def twice(col):
    return jnp.concatenate([col, col], axis=1)


def neighbours():
    time, region = lax.axis_index("time"), lax.axis_index("region")
    mate = {"batch": 0, "time": time, "region": region + 1 - 2 * (region % 2)}
    across = {"batch": 0, "time": time, "region": (region + 2) % 4}
    along = {"batch": 0, "time": 1 - time, "region": region}
    return mate, across, along


def greet(peers):
    for peer in peers:
        pl.semaphore_signal(pltpu.get_barrier_semaphore(), inc=1, device_id=peer, device_id_type=MESH)


def greeted(peers):
    pl.semaphore_wait(pltpu.get_barrier_semaphore(), len(peers))


def push(src, dst, send, recv, peer):
    return pltpu.make_async_remote_copy(src_ref=src, dst_ref=dst, send_sem=send, recv_sem=recv, device_id=peer, device_id_type=MESH)


class Gather:
    def __init__(self, src, slots, send, recv):
        self.mate, self.across, self.along = neighbours()
        half = slots.shape[1] // 2
        top, low = pl.ds(0, half), pl.ds(half, half)
        c = lambda i, s, d, peer: push(s, d, send.at[i], recv.at[i], peer)
        self.first = [c(0, src, slots.at[1], self.mate), c(1, src, slots.at[2], self.across), c(2, src, slots.at[4], self.along)]
        self.from_x = [c(3, slots.at[2, top], slots.at[6, top], self.along), c(4, slots.at[2], slots.at[3], self.mate)]
        self.from_y = [c(5, slots.at[4, low], slots.at[6, low], self.across), c(6, slots.at[4], slots.at[5], self.mate)]
        self.last = [c(7, slots.at[6, top], slots.at[7, top], self.mate), c(8, slots.at[6, low], slots.at[7, low], self.mate)]

    def start(self):
        for copy in self.first:
            copy.start()

    def relay(self):
        self.first[1].wait_recv()
        for copy in self.from_x:
            copy.start()
        self.first[2].wait_recv()
        for copy in self.from_y:
            copy.start()

    def relay_last(self):
        self.from_x[0].wait_recv()
        self.last[0].start()
        self.from_y[0].wait_recv()
        self.last[1].start()

    def finish(self):
        for copy in (self.first[0], self.from_x[1], self.from_y[1], *self.last):
            copy.wait_recv()

    def drain(self):
        for copy in (*self.first, *self.from_x, *self.from_y, *self.last):
            copy.wait_send()


def encoder_kernel(patches, enc_pos, mask, dec_pos, b_embed, vec, fin, w_embed, w_qkv, w_o, w_one, w_two, w_dec,
                   z_out, dall,
                   wemb, wqkv, wo, w1, w2, wdec, ebuf, drecv, csum, xrecv, hb, h, a, qkv, att, g, xs, xr, dsrc, bcol,
                   wsem, esend, erecv, xsend, xrecvs, gsend, grecv, osem):
    layers = w_qkv.shape[0]
    core = lax.axis_index("region") % 2
    mate, across, along = peers = neighbours()
    width = h.shape[1]
    heads = 8
    part = att.shape[0]
    dim = part // heads
    hid = w1.shape[2]
    feats = pl.ds(pl.multiple_of(core * part, LANES), part)
    hids = pl.ds(pl.multiple_of(core * hid, LANES), hid)
    chunks = width // TOK
    groups = [(0, 1), (2, 3), (4,)]

    load_embed = pltpu.make_async_copy(w_embed, wemb, wsem.at[0])
    load_embed.start()
    greet(peers)

    mrow = mask[:].astype(F32).astype(BF16)
    tok = mrow.shape[1]
    row_id = lax.broadcasted_iota(jnp.int32, (tok, tok), 0)
    col_id = lax.broadcasted_iota(jnp.int32, (tok, tok), 1)
    upper = (row_id <= col_id).astype(F32).astype(BF16)
    lower = (row_id >= col_id).astype(F32).astype(BF16)
    same = (row_id == col_id).astype(F32).astype(BF16)
    mrows = jnp.broadcast_to(mrow, (LANES, tok))
    rank = mm(mrows, upper)
    slot = lax.broadcasted_iota(jnp.int32, (LANES, tok), 0).astype(F32) + 1.0
    sel_f = jnp.where((rank == slot) & (mrows.astype(F32) > 0.5), 1.0, 0.0)
    sel = sel_f.astype(BF16)
    valid = jnp.sum(sel_f, axis=1, keepdims=True) > 0.5
    picked = mm(sel, patches[:]).astype(BF16)

    load_embed.wait()
    loads = {}
    k = 1
    for l in range(layers):
        for w in range(3):
            loads["qkv", l, w] = pltpu.make_async_copy(w_qkv.at[l, w, feats], wqkv.at[l, pl.ds(w * part, part)], wsem.at[k + w])
        loads["o", l] = pltpu.make_async_copy(w_o.at[l, feats], wo.at[l], wsem.at[k + 3])
        loads["one", l] = pltpu.make_async_copy(w_one.at[l, :, hids], w1.at[l], wsem.at[k + 4])
        loads["two", l] = pltpu.make_async_copy(w_two.at[l, hids], w2.at[l], wsem.at[k + 5])
        k += 6
    loads["dec"] = pltpu.make_async_copy(w_dec, wdec, wsem.at[k])
    for load in loads.values():
        load.start()

    pairs, xs1, ys1, f1, f2 = [], [], [], [], []
    for j in range(chunks):
        pairs.append(push(ebuf.at[j, 1 - core], drecv.at[j], esend.at[0, j], erecv.at[0, j], mate))
        xs1.append(push(csum.at[j], xrecv.at[j], esend.at[1, j], erecv.at[1, j], across))
        ys1.append(push(hb.at[0, core, j], hb.at[1, core, j], esend.at[2, j], erecv.at[2, j], along))
        f1.append(push(hb.at[0, core, j], hb.at[0, core, j], esend.at[3, j], erecv.at[3, j], mate))
        f2.append(push(hb.at[1, core, j], hb.at[1, core, j], esend.at[4, j], erecv.at[4, j], mate))
    for group in groups:
        cols = slice(TOK * group[0], TOK * (group[-1] + 1))
        e = mm(picked, wemb[:, cols]) + b_embed[cols].reshape(1, -1) + mm(sel, enc_pos[:, cols])
        e = jnp.where(valid, e, 0.0).astype(BF16)
        for i, j in enumerate(group):
            ebuf[j, 0] = e[:, TOK * i:TOK * i + LANES]
            ebuf[j, 1] = e[:, TOK * i + LANES:TOK * (i + 1)]
        if group[0] == 0:
            greeted(peers)
        for j in group:
            pairs[j].start()
    for j in range(chunks):
        pairs[j].wait_recv()
        csum[j] = ebuf[j, core] + drecv[j]
        xs1[j].start()
    code = mm(lower, mrows, NT) * mm(same, mrows, NT)
    dsrc[:, 0:DEC] = dec_pos[:]
    dsrc[:, DEC:CODED] = code.astype(BF16)
    for l in range(layers):
        bcol[l, 0] = column(vec[4, l:l + 1, feats])
        bcol[l, 1] = column(vec[5, l:l + 1, feats])
    for j in range(chunks):
        xs1[j].wait_recv()
        hb[0, core, j] = csum[j] + xrecv[j]
        ys1[j].start()
        f1[j].start()
    for j in range(chunks):
        ys1[j].wait_recv()
        f2[j].start()
    in_f1 = [push(hb.at[0, 1 - core, j], hb.at[0, 1 - core, j], esend.at[3, j], erecv.at[3, j], mate) for j in range(chunks)]
    in_f2 = [push(hb.at[1, 1 - core, j], hb.at[1, 1 - core, j], esend.at[4, j], erecv.at[4, j], mate) for j in range(chunks)]
    for j in range(chunks):
        in_f1[j].wait_recv()
        in_f2[j].wait_recv()
    for j in range(chunks):
        for copy in (pairs[j], xs1[j], ys1[j], f1[j], f2[j]):
            copy.wait_send()

    gather = Gather(dsrc, dall, gsend, grecv)
    own = pltpu.make_async_copy(dsrc, dall.at[0], osem.at[0])
    own.start()
    gather.start()

    for t in range(2):
        for half in range(2):
            for j in range(chunks):
                h[LANES * t:LANES * (t + 1), TOK * j + LANES * half:TOK * j + LANES * half + LANES] = hb[t, half, j]

    def exchange(slot):
        return [push(xs.at[slot, j], xr.at[slot, j], xsend.at[slot, j], xrecvs.at[slot, j], mate) for j in range(chunks)]

    def partials(slot, l, lhs, weights, dims):
        copies = exchange(slot)
        if l > 0:
            for copy in copies:
                copy.wait_send()
        for group in groups:
            r = mm(lhs[:], weights[l, :, TOK * group[0]:TOK * (group[-1] + 1)], dims)
            for i, j in enumerate(group):
                xs[slot, j] = r[:, TOK * i:TOK * (i + 1)]
            for j in group:
                copies[j].start()
        return copies

    def add_partials(slot, copies, bias):
        for j in range(chunks):
            cols = slice(TOK * j, TOK * (j + 1))
            copies[j].wait_recv()
            h[:, cols] = (h[:, cols].astype(F32) + (xs[slot, j] + xr[slot, j]) + bias[:, cols]).astype(BF16)

    def scores(hd):
        rows = slice(hd * dim, (hd + 1) * dim)
        return mm(qkv[part + hd * dim:part + (hd + 1) * dim, :], qkv[rows, :], TN)

    for l in range(layers):
        norm_rows(h, a, vec[0, l:l + 1, :], vec[1, l:l + 1, :], 64)
        for w in range(3):
            loads["qkv", l, w].wait()
        mid = 3 * part // 2
        low = mm(wqkv[l, :mid], a[:], NT)
        top = mm(wqkv[l, mid:], a[:], NT)
        qkv[:part, :] = (low[:part] + twice(bcol[l, 0])).astype(BF16)
        qkv[part:mid, :] = low[part:].astype(BF16)
        qkv[mid:2 * part, :] = top[:2 * part - mid].astype(BF16)
        qkv[2 * part:, :] = (top[2 * part - mid:] + twice(bcol[l, 1])).astype(BF16)
        scale = dim ** -0.5 * LOG2E
        s = scores(0)
        for hd in range(heads):
            nxt = scores(hd + 1) if hd + 1 < heads else None
            p = jnp.exp2(s * scale - jnp.max(s, axis=0, keepdims=True) * scale)
            total = jnp.sum(p, axis=0, keepdims=True)
            o = mm(qkv[2 * part + hd * dim:2 * part + (hd + 1) * dim, :], p.astype(BF16))
            att[hd * dim:(hd + 1) * dim, :] = (o * (1.0 / total)).astype(BF16)
            s = nxt
        loads["o", l].wait()
        copies = partials(0, l, att, wo, TN)
        if l > 0:
            gather.relay_last()
        add_partials(0, copies, vec[6, l:l + 1, :])
        norm_rows(h, a, vec[2, l:l + 1, :], vec[3, l:l + 1, :], 64)
        loads["one", l].wait()
        for j in range(hid // TOK):
            cols = slice(TOK * j, TOK * (j + 1))
            at = (TOK * j) % width
            bias = vec[8 + (hid // width) * core + (TOK * j) // width, l:l + 1, at:at + TOK]
            g[:, cols] = gelu(mm(a[:], w1[l, :, cols]) + bias).astype(BF16)
        if l == 0:
            gather.relay()
        loads["two", l].wait()
        copies = partials(1, l, g, w2, NN)
        add_partials(1, copies, vec[7, l:l + 1, :])
    norm_rows(h, a, fin[0:1, :], fin[1:2, :], 64)
    loads["dec"].wait()
    z_out[:] = mm(a[:], wdec[:]).astype(BF16)
    for slot in range(2):
        for copy in exchange(slot):
            copy.wait_send()
    gather.finish()
    gather.drain()
    own.wait()


def attend(q, kt, vt, att, buf, peak, state, dim, tiles, first, last, between=None):
    scale = dim ** -0.5 * LOG2E
    heads = att.shape[0] // dim
    tops, sums, outs = state

    def rows_of(hd):
        return pl.ds(pl.multiple_of(hd * dim, dim), dim)

    def step(score_hd, score_slot, hd, slot):
        best = jnp.full((8, TOK), -jnp.inf, F32)
        if hd is not None:
            top = jnp.max(peak[slot], axis=0, keepdims=True)
            if first:
                total = jnp.zeros((8, TOK), F32)
                out = jnp.zeros((dim, TOK), F32)
            else:
                old = tops[hd]
                top = jnp.maximum(old[0:1], top)
                fade = jnp.exp2((old[0:1] - top) * scale)
                total = sums[hd] * fade
                out = outs[rows_of(hd), :] * fade
            base = top * scale
        for i, tile in enumerate(tiles):
            keys, cols = slice(TOK * i, TOK * (i + 1)), slice(TOK * tile, TOK * (tile + 1))
            if score_hd is not None:
                s = mm(kt[rows_of(score_hd), cols], q[rows_of(score_hd), :], TN)
                buf[score_slot][keys, :] = s
                best = jnp.maximum(best, jnp.max(s.reshape(-1, 8, TOK), axis=0))
            if hd is not None:
                p = jnp.exp2(buf[slot][keys, :] * scale - base)
                total = total + jnp.sum(p.reshape(-1, 8, TOK), axis=0)
                out = out + mm(vt[rows_of(hd), cols], p.astype(BF16))
        if score_hd is not None:
            peak[score_slot] = best
        if hd is not None:
            if last:
                total = jnp.sum(total, axis=0, keepdims=True)
                att[rows_of(hd), :] = (out * (1.0 / total)).astype(BF16)
            else:
                tops[hd] = jnp.broadcast_to(top, (8, TOK))
                sums[hd] = total
                outs[rows_of(hd), :] = out

    def body(i, _):
        step(2 * i + 1, 1, 2 * i, 0)
        step(2 * i + 2, 0, 2 * i + 1, 1)
        return 0

    step(0, 0, None, None)
    half = heads // 4
    lax.fori_loop(0, half, body, 0)
    if between:
        between()
    lax.fori_loop(half, heads // 2 - 1, body, 0)
    step(heads - 1, 1, heads - 2, 0)
    step(None, None, heads - 1, 1)


def block_tail(h, att, a, g, vec, l, wo, w1, w2):
    h[:] = (h[:].astype(F32) + mm(att[:], wo[l], TN) + vec[6, l:l + 1, :]).astype(BF16)
    norm_rows(h, a, vec[2, l:l + 1, :], vec[3, l:l + 1, :], LANES)
    width = h.shape[1]
    for j in range(w1.shape[2] // width):
        cols = slice(width * j, width * (j + 1))
        g[:, cols] = gelu(mm(a[:], w1[l, :, cols]) + vec[8 + j, l:l + 1, :]).astype(BF16)
    h[:] = (h[:].astype(F32) + mm(g[:], w2[l]) + vec[7, l:l + 1, :]).astype(BF16)


def decoder_kernel(z, token, vec, fin, dall, w_qkv, w_o, w_one, w_two, y_out,
                   wqkv, wo, w1, w2, dslots, h, a, own, aall, arecv, kt, vt, q, att, g, buf0, buf1, peak, tops, sums, outs, bcol,
                   wsem, dsem, gsend, grecv):
    width = h.shape[1]
    layers = wqkv.shape[0]
    slots = dslots.shape[0]
    peers = neighbours()
    greet(peers)
    blocks = [pltpu.make_async_copy(dall.at[i], dslots.at[i], dsem.at[i]) for i in range(slots)]
    pairs = ((w_qkv, wqkv), (w_o, wo), (w_one, w1), (w_two, w2))
    loads = [[pltpu.make_async_copy(src.at[l], dst.at[l], wsem.at[l, i]) for i, (src, dst) in enumerate(pairs)] for l in range(layers)]
    loads[0][0].start()
    for block in blocks:
        block.start()

    for l in range(layers):
        bcol[l, 0] = column(vec[4, l:l + 1, :])
        bcol[l, 1] = column(vec[5, l:l + 1, :])
    lane = lax.broadcasted_iota(jnp.int32, (TOK, LANES), 1).astype(F32) + 1.0
    buf, state = (buf0, buf1), (tops, sums, outs)

    def queries(l, rows):
        q[:] = (mm(wqkv[l, 0:width, :], rows, NT) + twice(bcol[l, 0])).astype(BF16)

    def keys_values(l, i):
        cols = slice(TOK * i, TOK * (i + 1))
        rows = aall[i] if l == 0 else arecv[i]
        kt[:, cols] = mm(wqkv[l, width:2 * width, :], rows, NT).astype(BF16)
        vt[:, cols] = (mm(wqkv[l, 2 * width:, :], rows, NT) + twice(bcol[l, 1])).astype(BF16)

    def rows_in(i):
        code = dslots[i, :, DEC:CODED].astype(F32)
        pick = jnp.where(code == lane, 1.0, 0.0).astype(BF16)
        block = 0 if i < slots // 2 else LANES
        placed = mm(pick, z[block:block + LANES, :])
        seen = code[:, 0:1] > 0.5
        u = (jnp.where(seen, placed, token[:].astype(F32).reshape(1, -1)) + dslots[i, :, 0:DEC].astype(F32)).astype(BF16)
        if i == 0:
            h[:] = u
        aall[i] = norm(u.astype(F32), vec[0, 0:1, :], vec[1, 0:1, :]).astype(BF16)

    for block in blocks:
        block.wait()
    loads[0][0].wait()
    for load in loads[0][1:] + loads[1]:
        load.start()
    rows_in(0)
    queries(0, aall[0])
    for i in range(slots):
        keys_values(0, i)
        if i + 1 < slots:
            rows_in(i + 1)
    attend(q, kt, vt, att, buf, peak, state, width // 16, range(slots), True, True)
    for load in loads[0][1:]:
        load.wait()
    block_tail(h, att, a, g, vec, 0, wo, w1, w2)
    norm_rows(h, own, vec[0, 1:2, :], vec[1, 1:2, :], LANES)
    greeted(peers)
    gather = Gather(own, arecv, gsend, grecv)
    gather.start()
    arecv[0] = own[:]
    loads[1][0].wait()
    queries(1, own[:])
    keys_values(1, 0)
    gather.first[0].wait_recv()
    keys_values(1, 1)
    attend(q, kt, vt, att, buf, peak, state, width // 16, (0, 1), True, False)
    gather.relay()
    keys_values(1, 2)
    keys_values(1, 4)
    gather.from_x[1].wait_recv()
    keys_values(1, 3)
    gather.from_y[1].wait_recv()
    keys_values(1, 5)
    attend(q, kt, vt, att, buf, peak, state, width // 16, (2, 3, 4, 5), False, False, gather.relay_last)
    keys_values(1, 6)
    for copy in gather.last:
        copy.wait_recv()
    keys_values(1, 7)
    attend(q, kt, vt, att, buf, peak, state, width // 16, (6, 7), False, True)
    for load in loads[1][1:]:
        load.wait()
    block_tail(h, att, a, g, vec, 1, wo, w1, w2)
    norm_rows(h, y_out, fin[0:1, :], fin[1:2, :], LANES)
    gather.drain()


VM = pl.BlockSpec(memory_space=pltpu.VMEM)
HB = pl.BlockSpec(memory_space=pl.ANY)


def solution(mesh):
    def local_step(patches, enc_pos, vis_mask, dec_pos, w_embed, b_embed, enc_vec, enc_wqkv, enc_wo, enc_w1, enc_w2, enc_final, w_dec_in, mask_token, dec_vec, dec_wqkv, dec_wo, dec_w1, dec_w2, dec_final, w_out):
        layers = enc_vec.shape[0]
        evec = jnp.transpose(enc_vec, (1, 0, 2))
        dvec = jnp.transpose(dec_vec, (1, 0, 2))
        ewqkv = jnp.transpose(enc_wqkv, (0, 2, 3, 4, 1)).reshape(layers, 3, ENC, ENC)
        ewo = enc_wo.reshape(layers, ENC, ENC)
        dwqkv = jnp.transpose(dec_wqkv, (0, 2, 3, 4, 1)).reshape(layers, ALL, DEC)
        dwo = dec_wo.reshape(layers, DEC, DEC)
        dma = pltpu.SemaphoreType.DMA
        chunks = ENC // TOK
        piece = (chunks, LANES, LANES)
        z, dall = pl.pallas_call(
            encoder_kernel,
            out_shape=(jax.ShapeDtypeStruct((TOK, DEC), BF16), jax.ShapeDtypeStruct((8, TOK, CODED), BF16)),
            in_specs=[VM] * 7 + [HB] * 6,
            out_specs=(VM, HB),
            scratch_shapes=[
                vm(ALL, ENC),
                vm(layers, 3 * PART, ENC), vm(layers, PART, ENC), vm(layers, ENC, HID), vm(layers, HID, ENC), vm(ENC, DEC),
                vm(chunks, 2, LANES, LANES), vm(*piece), vm(*piece), vm(*piece), vm(2, 2, *piece),
                vm(TOK, ENC), vm(TOK, ENC), vm(3 * PART, TOK), vm(PART, TOK), vm(TOK, HID),
                vmf(2, chunks, TOK, TOK), vmf(2, chunks, TOK, TOK), vm(TOK, CODED), vmf(layers, 2, PART, LANES),
                dma((14,)), dma((chunks, chunks)), dma((chunks, chunks)), dma((2, chunks)), dma((2, chunks)), dma((9,)), dma((9,)), dma((1,)),
            ],
            compiler_params=pltpu.CompilerParams(collective_id=0, has_side_effects=True, vmem_limit_bytes=BIG),
            name="encoder",
        )(patches, enc_pos, vis_mask.reshape(1, -1), dec_pos, b_embed, evec, enc_final, w_embed, ewqkv, ewo, enc_w1, enc_w2, w_dec_in)
        y = pl.pallas_call(
            decoder_kernel,
            out_shape=jax.ShapeDtypeStruct((TOK, DEC), BF16),
            in_specs=[VM] * 4 + [HB] * 5,
            out_specs=VM,
            scratch_shapes=[
                vm(layers, ALL, DEC), vm(layers, DEC, DEC), vm(layers, DEC, KEYS), vm(layers, KEYS, DEC),
                vm(8, TOK, CODED), vm(TOK, DEC), vm(TOK, DEC), vm(TOK, DEC), vm(8, TOK, DEC), vm(8, TOK, DEC),
                vm(DEC, KEYS), vm(DEC, KEYS), vm(DEC, TOK), vm(DEC, TOK), vm(TOK, KEYS),
                vmf(KEYS, TOK), vmf(KEYS, TOK), vmf(2, 8, TOK), vmf(16, 8, TOK), vmf(16, 8, TOK), vmf(DEC, TOK), vmf(layers, 2, DEC, LANES),
                dma((layers, 4)), dma((8,)), dma((9,)), dma((9,)),
            ],
            compiler_params=pltpu.CompilerParams(collective_id=1, has_side_effects=True, vmem_limit_bytes=MID),
            name="decoder",
        )(z, mask_token, dvec, dec_final, dall, dwqkv, dwo, dec_w1, dec_w2)
        return jnp.dot(y, w_out, preferred_element_type=F32)

    token_rows = P(TOKEN_AXES, None)
    in_specs = (token_rows, token_rows, P(TOKEN_AXES), token_rows) + (P(),) * 17
    return jax.shard_map(local_step, mesh=mesh, in_specs=in_specs, out_specs=token_rows, check_vma=False)
```

time: 120 us -> 94.8 us (0.79)
  Pallas kernels: 114 us -> 91.8 us
  local copies, waits for them, and re-layouts: 2.57 us -> 0.01 us
    pallas_call x2 -> x1, Pallas kernels: 57.6 us -> 46.1 us  [local_step(): pl.pallas_call(decoder_kernel, out_shape=jax.ShapeDtypeStruct((TOK, DEC),...]
    pallas_call x1, Pallas kernels: 56.3 us -> 45.8 us  [local_step(): pl.pallas_call(encoder_kernel, out_shape=(jax.ShapeDtypeStruct((TOK, DEC)...]
    reshape x2 -> x0, local copies, waits for them, and re-layouts: 2.56 us -> none  [the longest x1 1.29 us: local_step(): b_embed.reshape(1, -1)]
where the time goes in v2:
time: 94.8 us; the launch traced here: 94.6 us
  Pallas kernels  91.8 us (97%)
  matrix products  2.67 us (3%)
    pallas_call x1, Pallas kernels, local_step(): pl.pallas_call(decoder_kernel, out_shape=jax.ShapeDtypeStruct((TOK, DEC),...  46.1 us
    pallas_call x1, Pallas kernels, local_step(): pl.pallas_call(encoder_kernel, out_shape=(jax.ShapeDtypeStruct((TOK, DEC)...  45.8 us
    dot_general x1, matrix products, local_step(): return jnp.dot(y, w_out, preferred_element_type=F32)  2.67 us

profile of v2, /device:TPU:0, one launch (start us, length us, event | category | flops | bytes accessed | tf_op | source)
XLA Modules:
  0.0 94.6 jit_solution(12876224503397237540)
XLA Ops:
  0.0 45.8 %encoder.1 = (bf16[256,512]{1,0:T(8,128)(2,1)}, bf16[8,256,640]{2,1,0:T(8,128)(2,1)}) custom-call(bf16[256,1536]{1,0:T(8,128)(2,1)} %patches.1, bf16[256,1280]{1,0:T(8,128)(2,1)} %enc_pos.1, s32[1,256]{1,0:T(1,128)} %bitcast.19, bf16[256,512]{1,0:T(8,128)(2,1)} %dec_pos.1, f32[1280]{0:T(1024)} %b_embed.1, f32[12,2,1280]{2,1,0:T(2,128)} %bitcast.17, ...), custom_call_target="tpu_custom_call" | custom-call | tf_op jit(solution)/shard_map/encoder/pallas_call | solution.py:470
  45.8 0.0 copy-start
  45.8 46.1 %decoder.1 = bf16[256,512]{1,0:T(8,128)(2,1)} custom-call(bf16[256,512]{1,0:T(8,128)(2,1)} %get-tuple-element.7.z, bf16[512]{0:T(512)(128)(2,1)} %token_.1, f32[12,2,512]{2,1,0:T(2,128)} %bitcast.18, f32[2,512]{1,0:T(2,128)} %fin.3, bf16[8,256,640]{2,1,0:T(8,128)(2,1)} %get-tuple-element.8.dall, bf16[2,1536,512]{2,1,0:T(8,128)(2,1)} %bitcast.15, ...), custom_call_target="tpu_custom_call" | custom-call | tf_op jit(solution)/shard_map/decoder/pallas_call | solution.py:486
  91.9 0.0 copy-done
  91.9 2.7 %fusion = f32[256,1536]{1,0:T(8,128)} fusion(bf16[256,512]{1,0:T(8,128)(2,1)} %decoder.1, bf16[512,1536]{1,0:T(8,128)(2,1)S(1)} %copy-done), kind=kOutput, calls=%fused_computation | convolution fusion | flops 402653184 | bytes 3407872 | tf_op jit(solution)/shard_map/dot_general | solution.py:501
Async XLA Ops:
  45.8 46.1 %copy-start = (bf16[512,1536]{1,0:T(8,128)(2,1)S(1)}, bf16[512,1536]{1,0:T(8,128)(2,1)}, u32[]{:S(2)}) copy-start(bf16[512,1536]{1,0:T(8,128)(2,1)} %param.41) | copy-start | bytes 4718596

commit v3 on v2

--- a/solution.py
+++ b/solution.py
@@ -16,6 +16,7 @@
 TN = (((0,), (0,)), ((), ()))
 NN = (((1,), (0,)), ((), ()))
 LOG2E = 1.4426950408889634
+TERMS, WIDE = 3, 16
 BIG, MID = 66_000_000, 60_000_000
 LANES, TOK, ENC, DEC = 128, 256, 1280, 512
 PART, HID, CODED, KEYS, ALL = 640, 2560, 640, 2048, 1536
@@ -119,8 +120,8 @@
 
 def encoder_kernel(patches, enc_pos, mask, dec_pos, b_embed, vec, fin, w_embed, w_qkv, w_o, w_one, w_two, w_dec,
                    z_out, dall,
-                   wemb, wqkv, wo, w1, w2, wdec, ebuf, drecv, csum, xrecv, hb, h, a, qkv, att, g, xs, xr, dsrc, bcol,
-                   wsem, esend, erecv, xsend, xrecvs, gsend, grecv, osem):
+                   wemb, wqkv, wo, w1, w2, wdec, vecs, ebuf, drecv, csum, xrecv, hb, h, a, qkv, att, g, xs, xr, dsrc, bcol,
+                   wsem, lsem, esend, erecv, xsend, xrecvs, gsend, grecv, osem):
     layers = w_qkv.shape[0]
     core = lax.axis_index("region") % 2
     mate, across, along = peers = neighbours()
@@ -154,18 +155,20 @@
     picked = mm(sel, patches[:]).astype(BF16)
 
     load_embed.wait()
-    loads = {}
-    k = 1
+
+    def layer_loads(l):
+        qkv_loads = [pltpu.make_async_copy(w_qkv.at[l, w, feats], wqkv.at[l, pl.ds(w * part, part)], lsem.at[l, w]) for w in range(3)]
+        return qkv_loads + [
+            pltpu.make_async_copy(w_o.at[l, feats], wo.at[l], lsem.at[l, 3]),
+            pltpu.make_async_copy(w_one.at[l, :, hids], w1.at[l], lsem.at[l, 4]),
+            pltpu.make_async_copy(w_two.at[l, hids], w2.at[l], lsem.at[l, 5]),
+        ]
+
+    load_dec = pltpu.make_async_copy(w_dec, wdec, wsem.at[1])
     for l in range(layers):
-        for w in range(3):
-            loads["qkv", l, w] = pltpu.make_async_copy(w_qkv.at[l, w, feats], wqkv.at[l, pl.ds(w * part, part)], wsem.at[k + w])
-        loads["o", l] = pltpu.make_async_copy(w_o.at[l, feats], wo.at[l], wsem.at[k + 3])
-        loads["one", l] = pltpu.make_async_copy(w_one.at[l, :, hids], w1.at[l], wsem.at[k + 4])
-        loads["two", l] = pltpu.make_async_copy(w_two.at[l, hids], w2.at[l], wsem.at[k + 5])
-        k += 6
-    loads["dec"] = pltpu.make_async_copy(w_dec, wdec, wsem.at[k])
-    for load in loads.values():
-        load.start()
+        for load in layer_loads(l):
+            load.start()
+    load_dec.start()
 
     pairs, xs1, ys1, f1, f2 = [], [], [], [], []
     for j in range(chunks):
@@ -193,6 +196,7 @@
     dsrc[:, 0:DEC] = dec_pos[:]
     dsrc[:, DEC:CODED] = code.astype(BF16)
     for l in range(layers):
+        vecs[l] = vec[:, l, :]
         bcol[l, 0] = column(vec[4, l:l + 1, feats])
         bcol[l, 1] = column(vec[5, l:l + 1, feats])
     for j in range(chunks):
@@ -227,9 +231,12 @@
 
     def partials(slot, l, lhs, weights, dims):
         copies = exchange(slot)
-        if l > 0:
+
+        @pl.when(l > 0)
+        def _():
             for copy in copies:
                 copy.wait_send()
+
         for group in groups:
             r = mm(lhs[:], weights[l, :, TOK * group[0]:TOK * (group[-1] + 1)], dims)
             for i, j in enumerate(group):
@@ -248,10 +255,14 @@
         rows = slice(hd * dim, (hd + 1) * dim)
         return mm(qkv[part + hd * dim:part + (hd + 1) * dim, :], qkv[rows, :], TN)
 
-    for l in range(layers):
-        norm_rows(h, a, vec[0, l:l + 1, :], vec[1, l:l + 1, :], 64)
-        for w in range(3):
-            loads["qkv", l, w].wait()
+    def layer(l, _):
+        def row(i):
+            return vecs[l, i:i + 1, :]
+
+        *qkv_loads, load_o, load_one, load_two = layer_loads(l)
+        norm_rows(h, a, row(0), row(1), 64)
+        for load in qkv_loads:
+            load.wait()
         mid = 3 * part // 2
         low = mm(wqkv[l, :mid], a[:], NT)
         top = mm(wqkv[l, mid:], a[:], NT)
@@ -268,25 +279,27 @@
             o = mm(qkv[2 * part + hd * dim:2 * part + (hd + 1) * dim, :], p.astype(BF16))
             att[hd * dim:(hd + 1) * dim, :] = (o * (1.0 / total)).astype(BF16)
             s = nxt
-        loads["o", l].wait()
+        load_o.wait()
         copies = partials(0, l, att, wo, TN)
-        if l > 0:
-            gather.relay_last()
-        add_partials(0, copies, vec[6, l:l + 1, :])
-        norm_rows(h, a, vec[2, l:l + 1, :], vec[3, l:l + 1, :], 64)
-        loads["one", l].wait()
+        pl.when(l > 0)(gather.relay_last)
+        add_partials(0, copies, row(6))
+        norm_rows(h, a, row(2), row(3), 64)
+        load_one.wait()
+        wide_bias = [vecs[l, pl.ds(8 + (hid // width) * core + i, 1), :] for i in range(hid // width)]
         for j in range(hid // TOK):
             cols = slice(TOK * j, TOK * (j + 1))
             at = (TOK * j) % width
-            bias = vec[8 + (hid // width) * core + (TOK * j) // width, l:l + 1, at:at + TOK]
+            bias = wide_bias[(TOK * j) // width][:, at:at + TOK]
             g[:, cols] = gelu(mm(a[:], w1[l, :, cols]) + bias).astype(BF16)
-        if l == 0:
-            gather.relay()
-        loads["two", l].wait()
+        pl.when(l == 0)(gather.relay)
+        load_two.wait()
         copies = partials(1, l, g, w2, NN)
-        add_partials(1, copies, vec[7, l:l + 1, :])
+        add_partials(1, copies, row(7))
+        return 0
+
+    lax.fori_loop(0, layers, layer, 0)
     norm_rows(h, a, fin[0:1, :], fin[1:2, :], 64)
-    loads["dec"].wait()
+    load_dec.wait()
     z_out[:] = mm(a[:], wdec[:]).astype(BF16)
     for slot in range(2):
         for copy in exchange(slot):
@@ -297,47 +310,57 @@
 
 
 def attend(q, kt, vt, att, buf, peak, state, dim, tiles, first, last, between=None):
-    scale = dim ** -0.5 * LOG2E
-    heads = att.shape[0] // dim
+    deep = TERMS * dim
     tops, sums, outs = state
-
-    def rows_of(hd):
-        return pl.ds(pl.multiple_of(hd * dim, dim), dim)
-
-    def step(score_hd, score_slot, hd, slot):
-        best = jnp.full((8, TOK), -jnp.inf, F32)
-        if hd is not None:
-            top = jnp.max(peak[slot], axis=0, keepdims=True)
-            if first:
-                total = jnp.zeros((8, TOK), F32)
-                out = jnp.zeros((dim, TOK), F32)
-            else:
-                old = tops[hd]
-                top = jnp.maximum(old[0:1], top)
-                fade = jnp.exp2((old[0:1] - top) * scale)
-                total = sums[hd] * fade
-                out = outs[rows_of(hd), :] * fade
-            base = top * scale
-        for i, tile in enumerate(tiles):
-            keys, cols = slice(TOK * i, TOK * (i + 1)), slice(TOK * tile, TOK * (tile + 1))
-            if score_hd is not None:
-                s = mm(kt[rows_of(score_hd), cols], q[rows_of(score_hd), :], TN)
-                buf[score_slot][keys, :] = s
-                best = jnp.maximum(best, jnp.max(s.reshape(-1, 8, TOK), axis=0))
-            if hd is not None:
-                p = jnp.exp2(buf[slot][keys, :] * scale - base)
-                total = total + jnp.sum(p.reshape(-1, 8, TOK), axis=0)
-                out = out + mm(vt[rows_of(hd), cols], p.astype(BF16))
-        if score_hd is not None:
-            peak[score_slot] = best
-        if hd is not None:
-            if last:
-                total = jnp.sum(total, axis=0, keepdims=True)
-                att[rows_of(hd), :] = (out * (1.0 / total)).astype(BF16)
-            else:
-                tops[hd] = jnp.broadcast_to(top, (8, TOK))
-                sums[hd] = total
-                outs[rows_of(hd), :] = out
+    crew = max(1, WIDE // len(tiles))
+    units = att.shape[0] // dim // crew
+
+    def rows_of(hd, size):
+        start = hd * size
+        return pl.ds(start if isinstance(start, int) else pl.multiple_of(start, size), size)
+
+    def begin(hd, spot):
+        top = jnp.max(peak[spot], axis=0, keepdims=True)
+        if first:
+            return top, jnp.zeros((8, TOK), F32), jnp.zeros((dim, TOK), F32)
+        old = tops[hd]
+        top = jnp.maximum(old[0:1], top)
+        fade = jnp.exp2(old[0:1] - top)
+        return top, sums[hd] * fade, outs[rows_of(hd, dim), :] * fade
+
+    def end(hd, top, total, out):
+        if last:
+            total = jnp.sum(total, axis=0, keepdims=True)
+            att[rows_of(hd, dim), :] = (out * (1.0 / total)).astype(BF16)
+        else:
+            tops[hd] = jnp.broadcast_to(top, (8, TOK))
+            sums[hd] = total
+            outs[rows_of(hd, dim), :] = out
+
+    def step(score_unit, score_slot, unit, slot):
+        best = [jnp.full((8, TOK), -jnp.inf, F32)] * crew
+        if unit is not None:
+            runs = [begin(unit * crew + n, slot * crew + n) for n in range(crew)]
+        for n in range(crew):
+            for i, tile in enumerate(tiles):
+                keys = slice(TOK * (n * len(tiles) + i), TOK * (n * len(tiles) + i + 1))
+                cols = slice(TOK * tile, TOK * (tile + 1))
+                if score_unit is not None:
+                    rows = rows_of(score_unit * crew + n, deep)
+                    s = mm(kt[rows, cols], q[rows, :], TN)
+                    buf[score_slot][keys, :] = s
+                    best[n] = jnp.maximum(best[n], jnp.max(s.reshape(-1, 8, TOK), axis=0))
+                if unit is not None:
+                    top, total, out = runs[n]
+                    p = jnp.exp2(buf[slot][keys, :] - top)
+                    total = total + jnp.sum(p.reshape(-1, 8, TOK), axis=0)
+                    out = out + mm(vt[rows_of(unit * crew + n, dim), cols], p.astype(BF16))
+                    runs[n] = top, total, out
+        for n in range(crew):
+            if score_unit is not None:
+                peak[score_slot * crew + n] = best[n]
+            if unit is not None:
+                end(unit * crew + n, *runs[n])
 
     def body(i, _):
         step(2 * i + 1, 1, 2 * i, 0)
@@ -345,23 +368,65 @@
         return 0
 
     step(0, 0, None, None)
-    half = heads // 4
+    half = units // 4
     lax.fori_loop(0, half, body, 0)
     if between:
         between()
-    lax.fori_loop(half, heads // 2 - 1, body, 0)
-    step(heads - 1, 1, heads - 2, 0)
-    step(None, None, heads - 1, 1)
-
-
-def block_tail(h, att, a, g, vec, l, wo, w1, w2):
-    h[:] = (h[:].astype(F32) + mm(att[:], wo[l], TN) + vec[6, l:l + 1, :]).astype(BF16)
-    norm_rows(h, a, vec[2, l:l + 1, :], vec[3, l:l + 1, :], LANES)
+    lax.fori_loop(half, units // 2 - 1, body, 0)
+    step(units - 1, 1, units - 2, 0)
+    step(None, None, units - 1, 1)
+
+
+def block_tail(h, att, a, g, vec, l, wo, w1, w2, rows):
+    h[rows, :] = (h[rows, :].astype(F32) + mm(att[:, rows], wo[l], TN) + vec[6, l:l + 1, :]).astype(BF16)
+    a[rows, :] = norm(h[rows, :].astype(F32), vec[2, l:l + 1, :], vec[3, l:l + 1, :]).astype(BF16)
     width = h.shape[1]
     for j in range(w1.shape[2] // width):
         cols = slice(width * j, width * (j + 1))
-        g[:, cols] = gelu(mm(a[:], w1[l, :, cols]) + vec[8 + j, l:l + 1, :]).astype(BF16)
-    h[:] = (h[:].astype(F32) + mm(g[:], w2[l]) + vec[7, l:l + 1, :]).astype(BF16)
+        g[rows, cols] = gelu(mm(a[rows, :], w1[l, :, cols]) + vec[8 + j, l:l + 1, :]).astype(BF16)
+    h[rows, :] = (h[rows, :].astype(F32) + mm(g[rows, :], w2[l]) + vec[7, l:l + 1, :]).astype(BF16)
+
+
+class Halves:
+    def __init__(self, src, tiles, send, recv):
+        self.mate, self.across, self.along = neighbours()
+        half = tiles.shape[1] // 2
+        top, low = pl.ds(0, half), pl.ds(half, half)
+        made = []
+
+        def c(s, d, peer):
+            made.append(push(s, d, send.at[len(made)], recv.at[len(made)], peer))
+            return made[-1]
+
+        self.own = [[c(src.at[r], tiles.at[2 + 2 * n, top], self.across), c(src.at[r], tiles.at[2 + 2 * n, low], self.along),
+                     c(src.at[r], tiles.at[1, r], self.mate)] for n, r in enumerate((top, low))]
+        self.mates = [[c(tiles.at[2 + 2 * n, r], tiles.at[3 + 2 * n, r], self.mate) for r in (top, low)] for n in range(3)]
+        self.corner = [c(tiles.at[2, top], tiles.at[6, top], self.along), c(tiles.at[4, low], tiles.at[6, low], self.across)]
+        self.made = made
+
+    def start(self, n):
+        for copy in self.own[n]:
+            copy.start()
+
+    def relay(self, n):
+        for i in range(2):
+            self.own[n][i].wait_recv()
+        self.corner[n].start()
+        for copy in self.mates[n]:
+            copy.start()
+
+    def relay_corner(self):
+        for n in range(2):
+            self.corner[n].wait_recv()
+            self.mates[2][n].start()
+
+    def from_mate(self, n):
+        for copy in self.mates[n]:
+            copy.wait_recv()
+
+    def drain(self):
+        for copy in self.made:
+            copy.wait_send()
 
 
 def decoder_kernel(z, token, vec, fin, dall, w_qkv, w_o, w_one, w_two, y_out,
@@ -385,13 +450,23 @@
     lane = lax.broadcasted_iota(jnp.int32, (TOK, LANES), 1).astype(F32) + 1.0
     buf, state = (buf0, buf1), (tops, sums, outs)
 
+    dim = width // 16
+
     def queries(l, rows):
-        q[:] = (mm(wqkv[l, 0:width, :], rows, NT) + twice(bcol[l, 0])).astype(BF16)
+        rest = (mm(wqkv[l, 0:width, :], rows, NT) + twice(bcol[l, 0])).astype(BF16).astype(F32) * (dim ** -0.5 * LOG2E)
+        for t in range(TERMS):
+            term = rest.astype(BF16)
+            rest = rest - term.astype(F32)
+            for hd in range(width // dim):
+                q[(TERMS * hd + t) * dim:(TERMS * hd + t + 1) * dim, :] = term[hd * dim:(hd + 1) * dim]
 
     def keys_values(l, i):
         cols = slice(TOK * i, TOK * (i + 1))
         rows = aall[i] if l == 0 else arecv[i]
-        kt[:, cols] = mm(wqkv[l, width:2 * width, :], rows, NT).astype(BF16)
+        key = mm(wqkv[l, width:2 * width, :], rows, NT).astype(BF16)
+        for hd in range(width // dim):
+            for t in range(TERMS):
+                kt[(TERMS * hd + t) * dim:(TERMS * hd + t + 1) * dim, cols] = key[hd * dim:(hd + 1) * dim]
         vt[:, cols] = (mm(wqkv[l, 2 * width:, :], rows, NT) + twice(bcol[l, 1])).astype(BF16)
 
     def rows_in(i):
@@ -416,37 +491,39 @@
         keys_values(0, i)
         if i + 1 < slots:
             rows_in(i + 1)
-    attend(q, kt, vt, att, buf, peak, state, width // 16, range(slots), True, True)
+    attend(q, kt, vt, att, buf, peak, state, dim, range(slots), True, True)
     for load in loads[0][1:]:
         load.wait()
-    block_tail(h, att, a, g, vec, 0, wo, w1, w2)
-    norm_rows(h, own, vec[0, 1:2, :], vec[1, 1:2, :], LANES)
-    greeted(peers)
-    gather = Gather(own, arecv, gsend, grecv)
-    gather.start()
+    gather = Halves(own, arecv, gsend, grecv)
+    ways = (slice(0, LANES), slice(LANES, TOK))
+    for n, rows in enumerate(ways):
+        block_tail(h, att, a, g, vec, 0, wo, w1, w2, rows)
+        own[rows, :] = norm(h[rows, :].astype(F32), vec[0, 1:2, :], vec[1, 1:2, :]).astype(BF16)
+        if n == 0:
+            greeted(peers)
+        gather.start(n)
     arecv[0] = own[:]
     loads[1][0].wait()
     queries(1, own[:])
     keys_values(1, 0)
-    gather.first[0].wait_recv()
+    for n in range(2):
+        gather.own[n][2].wait_recv()
     keys_values(1, 1)
-    attend(q, kt, vt, att, buf, peak, state, width // 16, (0, 1), True, False)
-    gather.relay()
-    keys_values(1, 2)
-    keys_values(1, 4)
-    gather.from_x[1].wait_recv()
-    keys_values(1, 3)
-    gather.from_y[1].wait_recv()
-    keys_values(1, 5)
-    attend(q, kt, vt, att, buf, peak, state, width // 16, (2, 3, 4, 5), False, False, gather.relay_last)
+    attend(q, kt, vt, att, buf, peak, state, dim, (0, 1), True, False)
+    for n in range(2):
+        gather.relay(n)
+        keys_values(1, 2 + 2 * n)
+        gather.from_mate(n)
+        keys_values(1, 3 + 2 * n)
+        attend(q, kt, vt, att, buf, peak, state, dim, (2 + 2 * n, 3 + 2 * n), False, False)
+    gather.relay_corner()
     keys_values(1, 6)
-    for copy in gather.last:
-        copy.wait_recv()
+    gather.from_mate(2)
     keys_values(1, 7)
-    attend(q, kt, vt, att, buf, peak, state, width // 16, (6, 7), False, True)
+    attend(q, kt, vt, att, buf, peak, state, dim, (6, 7), False, True)
     for load in loads[1][1:]:
         load.wait()
-    block_tail(h, att, a, g, vec, 1, wo, w1, w2)
+    block_tail(h, att, a, g, vec, 1, wo, w1, w2, slice(0, TOK))
     norm_rows(h, y_out, fin[0:1, :], fin[1:2, :], LANES)
     gather.drain()
 
@@ -474,11 +551,11 @@
             out_specs=(VM, HB),
             scratch_shapes=[
                 vm(ALL, ENC),
-                vm(layers, 3 * PART, ENC), vm(layers, PART, ENC), vm(layers, ENC, HID), vm(layers, HID, ENC), vm(ENC, DEC),
+                vm(layers, 3 * PART, ENC), vm(layers, PART, ENC), vm(layers, ENC, HID), vm(layers, HID, ENC), vm(ENC, DEC), vmf(layers, 12, ENC),
                 vm(chunks, 2, LANES, LANES), vm(*piece), vm(*piece), vm(*piece), vm(2, 2, *piece),
                 vm(TOK, ENC), vm(TOK, ENC), vm(3 * PART, TOK), vm(PART, TOK), vm(TOK, HID),
                 vmf(2, chunks, TOK, TOK), vmf(2, chunks, TOK, TOK), vm(TOK, CODED), vmf(layers, 2, PART, LANES),
-                dma((14,)), dma((chunks, chunks)), dma((chunks, chunks)), dma((2, chunks)), dma((2, chunks)), dma((9,)), dma((9,)), dma((1,)),
+                dma((2,)), dma((layers, 6)), dma((chunks, chunks)), dma((chunks, chunks)), dma((2, chunks)), dma((2, chunks)), dma((9,)), dma((9,)), dma((1,)),
             ],
             compiler_params=pltpu.CompilerParams(collective_id=0, has_side_effects=True, vmem_limit_bytes=BIG),
             name="encoder",
@@ -491,9 +568,9 @@
             scratch_shapes=[
                 vm(layers, ALL, DEC), vm(layers, DEC, DEC), vm(layers, DEC, KEYS), vm(layers, KEYS, DEC),
                 vm(8, TOK, CODED), vm(TOK, DEC), vm(TOK, DEC), vm(TOK, DEC), vm(8, TOK, DEC), vm(8, TOK, DEC),
-                vm(DEC, KEYS), vm(DEC, KEYS), vm(DEC, TOK), vm(DEC, TOK), vm(TOK, KEYS),
-                vmf(KEYS, TOK), vmf(KEYS, TOK), vmf(2, 8, TOK), vmf(16, 8, TOK), vmf(16, 8, TOK), vmf(DEC, TOK), vmf(layers, 2, DEC, LANES),
-                dma((layers, 4)), dma((8,)), dma((9,)), dma((9,)),
+                vm(TERMS * DEC, KEYS), vm(DEC, KEYS), vm(TERMS * DEC, TOK), vm(DEC, TOK), vm(TOK, KEYS),
+                vmf(WIDE * TOK, TOK), vmf(WIDE * TOK, TOK), vmf(WIDE, 8, TOK), vmf(16, 8, TOK), vmf(16, 8, TOK), vmf(DEC, TOK), vmf(layers, 2, DEC, LANES),
+                dma((layers, 4)), dma((8,)), dma((14,)), dma((14,)),
             ],
             compiler_params=pltpu.CompilerParams(collective_id=1, has_side_effects=True, vmem_limit_bytes=MID),
             name="decoder",

time: 94.8 us -> 86.8 us (0.916)
  Pallas kernels: 91.8 us -> 83.9 us
    pallas_call x1, Pallas kernels: 46.1 us -> 38.3 us  [local_step(): pl.pallas_call(decoder_kernel, out_shape=jax.ShapeDtypeStruct((TOK, DEC),...]
where the time goes in v3:
time: 86.8 us; the launch traced here: 86.6 us
  Pallas kernels  83.9 us (97%)
  matrix products  2.67 us (3%)
    pallas_call x1, Pallas kernels, local_step(): pl.pallas_call(encoder_kernel, out_shape=(jax.ShapeDtypeStruct((TOK, DEC)...  45.6 us
    pallas_call x1, Pallas kernels, local_step(): pl.pallas_call(decoder_kernel, out_shape=jax.ShapeDtypeStruct((TOK, DEC),...  38.3 us
    dot_general x1, matrix products, local_step(): return jnp.dot(y, w_out, preferred_element_type=F32)  2.67 us

profile of v3, /device:TPU:0, one launch (start us, length us, event | category | flops | bytes accessed | tf_op | source)
XLA Modules:
  0.0 86.6 jit_solution(632515196676326359)
XLA Ops:
  0.0 45.6 %encoder.1 = (bf16[256,512]{1,0:T(8,128)(2,1)}, bf16[8,256,640]{2,1,0:T(8,128)(2,1)}) custom-call(bf16[256,1536]{1,0:T(8,128)(2,1)} %patches.1, bf16[256,1280]{1,0:T(8,128)(2,1)} %enc_pos.1, s32[1,256]{1,0:T(1,128)} %bitcast.19, bf16[256,512]{1,0:T(8,128)(2,1)} %dec_pos.1, f32[1280]{0:T(1024)} %b_embed.1, f32[12,2,1280]{2,1,0:T(2,128)} %bitcast.17, ...), custom_call_target="tpu_custom_call" | custom-call | tf_op jit(solution)/shard_map/encoder/pallas_call | solution.py:547
  45.6 0.0 copy-start
  45.6 38.3 %decoder.1 = bf16[256,512]{1,0:T(8,128)(2,1)} custom-call(bf16[256,512]{1,0:T(8,128)(2,1)} %get-tuple-element.7.z, bf16[512]{0:T(512)(128)(2,1)} %token_.1, f32[12,2,512]{2,1,0:T(2,128)} %bitcast.18, f32[2,512]{1,0:T(2,128)} %fin.3, bf16[8,256,640]{2,1,0:T(8,128)(2,1)} %get-tuple-element.8.dall, bf16[2,1536,512]{2,1,0:T(8,128)(2,1)} %bitcast.15, ...), custom_call_target="tpu_custom_call" | custom-call | tf_op jit(solution)/shard_map/decoder/pallas_call | solution.py:563
  83.9 0.0 copy-done
  84.0 2.7 %fusion = f32[256,1536]{1,0:T(8,128)} fusion(bf16[256,512]{1,0:T(8,128)(2,1)} %decoder.1, bf16[512,1536]{1,0:T(8,128)(2,1)S(1)} %copy-done), kind=kOutput, calls=%fused_computation | convolution fusion | flops 402653184 | bytes 3407872 | tf_op jit(solution)/shard_map/dot_general | solution.py:578
Async XLA Ops:
  45.6 38.3 %copy-start = (bf16[512,1536]{1,0:T(8,128)(2,1)S(1)}, bf16[512,1536]{1,0:T(8,128)(2,1)}, u32[]{:S(2)}) copy-start(bf16[512,1536]{1,0:T(8,128)(2,1)} %param.41) | copy-start | bytes 4718596

commit v4 on v3

--- a/solution.py
+++ b/solution.py
@@ -17,7 +17,7 @@
 NN = (((1,), (0,)), ((), ()))
 LOG2E = 1.4426950408889634
 TERMS, WIDE = 3, 16
-BIG, MID = 66_000_000, 60_000_000
+BIG, MID = 66_000_000, 65_000_000
 LANES, TOK, ENC, DEC = 128, 256, 1280, 512
 PART, HID, CODED, KEYS, ALL = 640, 2560, 640, 2048, 1536
 
@@ -118,10 +118,10 @@
             copy.wait_send()
 
 
-def encoder_kernel(patches, enc_pos, mask, dec_pos, b_embed, vec, fin, w_embed, w_qkv, w_o, w_one, w_two, w_dec,
+def encoder_kernel(mask, b_embed, patches_in, enc_pos_in, dec_pos, vec_in, fin_in, w_embed, w_qkv, w_o, w_one, w_two, w_dec,
                    z_out, dall,
-                   wemb, wqkv, wo, w1, w2, wdec, vecs, ebuf, drecv, csum, xrecv, hb, h, a, qkv, att, g, xs, xr, dsrc, bcol,
-                   wsem, lsem, esend, erecv, xsend, xrecvs, gsend, grecv, osem):
+                   patches, enc_pos, vec, fin, wemb, wqkv, wo, w1, w2, wdec, vecs, ebuf, drecv, csum, xrecv, hb, h, a, low_a, qkv, att, peer_att, acc, g, dsrc, bcol,
+                   wsem, esem, lsem, esend, erecv, xsend, xrecvs, gsend, grecv, osem):
     layers = w_qkv.shape[0]
     core = lax.axis_index("region") % 2
     mate, across, along = peers = neighbours()
@@ -129,14 +129,21 @@
     heads = 8
     part = att.shape[0]
     dim = part // heads
-    hid = w1.shape[2]
     feats = pl.ds(pl.multiple_of(core * part, LANES), part)
-    hids = pl.ds(pl.multiple_of(core * hid, LANES), hid)
+    other_feats = pl.ds(pl.multiple_of((1 - core) * part, LANES), part)
+    mine = pl.ds(pl.multiple_of(core * LANES, LANES), LANES)
+    theirs = pl.ds(pl.multiple_of((1 - core) * LANES, LANES), LANES)
     chunks = width // TOK
     groups = [(0, 1), (2, 3), (4,)]
 
-    load_embed = pltpu.make_async_copy(w_embed, wemb, wsem.at[0])
-    load_embed.start()
+    spans = [slice(TOK * group[0], TOK * (group[-1] + 1)) for group in groups]
+    load_patches = pltpu.make_async_copy(patches_in, patches, wsem.at[2])
+    load_pos = pltpu.make_async_copy(enc_pos_in, enc_pos, wsem.at[3])
+    load_embed = [pltpu.make_async_copy(w_embed.at[:, span], wemb.at[:, span], esem.at[i]) for i, span in enumerate(spans)]
+    late = [pltpu.make_async_copy(vec_in, vec, wsem.at[4]), pltpu.make_async_copy(fin_in, fin, wsem.at[5]),
+            pltpu.make_async_copy(dec_pos, dsrc.at[:, pl.ds(0, DEC)], wsem.at[0])]
+    for load in (load_patches, load_embed[0], load_pos, *load_embed[1:], *late):
+        load.start()
     greet(peers)
 
     mrow = mask[:].astype(F32).astype(BF16)
@@ -152,23 +159,18 @@
     sel_f = jnp.where((rank == slot) & (mrows.astype(F32) > 0.5), 1.0, 0.0)
     sel = sel_f.astype(BF16)
     valid = jnp.sum(sel_f, axis=1, keepdims=True) > 0.5
+    load_patches.wait()
     picked = mm(sel, patches[:]).astype(BF16)
 
-    load_embed.wait()
-
     def layer_loads(l):
-        qkv_loads = [pltpu.make_async_copy(w_qkv.at[l, w, feats], wqkv.at[l, pl.ds(w * part, part)], lsem.at[l, w]) for w in range(3)]
+        qkv_loads = [pltpu.make_async_copy(w_qkv.at[l, w, feats], wqkv.at[pl.ds(w * part, part)], lsem.at[l, w]) for w in range(3)]
         return qkv_loads + [
-            pltpu.make_async_copy(w_o.at[l, feats], wo.at[l], lsem.at[l, 3]),
-            pltpu.make_async_copy(w_one.at[l, :, hids], w1.at[l], lsem.at[l, 4]),
-            pltpu.make_async_copy(w_two.at[l, hids], w2.at[l], lsem.at[l, 5]),
+            pltpu.make_async_copy(w_o.at[l], wo, lsem.at[l, 3]),
+            pltpu.make_async_copy(w_one.at[l], w1, lsem.at[l, 4]),
+            pltpu.make_async_copy(w_two.at[l], w2, lsem.at[l, 5]),
         ]
 
     load_dec = pltpu.make_async_copy(w_dec, wdec, wsem.at[1])
-    for l in range(layers):
-        for load in layer_loads(l):
-            load.start()
-    load_dec.start()
 
     pairs, xs1, ys1, f1, f2 = [], [], [], [], []
     for j in range(chunks):
@@ -177,8 +179,11 @@
         ys1.append(push(hb.at[0, core, j], hb.at[1, core, j], esend.at[2, j], erecv.at[2, j], along))
         f1.append(push(hb.at[0, core, j], hb.at[0, core, j], esend.at[3, j], erecv.at[3, j], mate))
         f2.append(push(hb.at[1, core, j], hb.at[1, core, j], esend.at[4, j], erecv.at[4, j], mate))
-    for group in groups:
-        cols = slice(TOK * group[0], TOK * (group[-1] + 1))
+    for n, group in enumerate(groups):
+        cols = spans[n]
+        load_embed[n].wait()
+        if n == 0:
+            load_pos.wait()
         e = mm(picked, wemb[:, cols]) + b_embed[cols].reshape(1, -1) + mm(sel, enc_pos[:, cols])
         e = jnp.where(valid, e, 0.0).astype(BF16)
         for i, j in enumerate(group):
@@ -188,13 +193,17 @@
             greeted(peers)
         for j in group:
             pairs[j].start()
+    for load in layer_loads(0):
+        load.start()
     for j in range(chunks):
         pairs[j].wait_recv()
         csum[j] = ebuf[j, core] + drecv[j]
         xs1[j].start()
     code = mm(lower, mrows, NT) * mm(same, mrows, NT)
-    dsrc[:, 0:DEC] = dec_pos[:]
     dsrc[:, DEC:CODED] = code.astype(BF16)
+    for load in late:
+        load.wait()
+    vecs[layers, 0:2, :] = fin[:]
     for l in range(layers):
         vecs[l] = vec[:, l, :]
         bcol[l, 0] = column(vec[4, l:l + 1, feats])
@@ -226,30 +235,11 @@
             for j in range(chunks):
                 h[LANES * t:LANES * (t + 1), TOK * j + LANES * half:TOK * j + LANES * half + LANES] = hb[t, half, j]
 
-    def exchange(slot):
-        return [push(xs.at[slot, j], xr.at[slot, j], xsend.at[slot, j], xrecvs.at[slot, j], mate) for j in range(chunks)]
-
-    def partials(slot, l, lhs, weights, dims):
-        copies = exchange(slot)
-
-        @pl.when(l > 0)
-        def _():
-            for copy in copies:
-                copy.wait_send()
-
-        for group in groups:
-            r = mm(lhs[:], weights[l, :, TOK * group[0]:TOK * (group[-1] + 1)], dims)
-            for i, j in enumerate(group):
-                xs[slot, j] = r[:, TOK * i:TOK * (i + 1)]
-            for j in group:
-                copies[j].start()
-        return copies
-
-    def add_partials(slot, copies, bias):
-        for j in range(chunks):
-            cols = slice(TOK * j, TOK * (j + 1))
-            copies[j].wait_recv()
-            h[:, cols] = (h[:, cols].astype(F32) + (xs[slot, j] + xr[slot, j]) + bias[:, cols]).astype(BF16)
+    half_att = part // 2
+    send_att = [push(att.at[pl.ds(i * half_att, half_att), theirs], peer_att.at[pl.ds(i * half_att, half_att)], xsend.at[2 + i], xrecvs.at[2 + i], mate)
+                for i in range(2)]
+    send_rows = push(a.at[mine], a.at[mine], xsend.at[1], xrecvs.at[1], mate)
+    get_rows = push(a.at[theirs], a.at[theirs], xsend.at[1], xrecvs.at[1], mate)
 
     def scores(hd):
         rows = slice(hd * dim, (hd + 1) * dim)
@@ -260,16 +250,22 @@
             return vecs[l, i:i + 1, :]
 
         *qkv_loads, load_o, load_one, load_two = layer_loads(l)
-        norm_rows(h, a, row(0), row(1), 64)
         for load in qkv_loads:
             load.wait()
         mid = 3 * part // 2
-        low = mm(wqkv[l, :mid], a[:], NT)
-        top = mm(wqkv[l, mid:], a[:], NT)
+        low = mm(wqkv[:mid, :], a[:], NT)
+        top = mm(wqkv[mid:, :], a[:], NT)
         qkv[:part, :] = (low[:part] + twice(bcol[l, 0])).astype(BF16)
         qkv[part:mid, :] = low[part:].astype(BF16)
         qkv[mid:2 * part, :] = top[:2 * part - mid].astype(BF16)
         qkv[2 * part:, :] = (top[2 * part - mid:] + twice(bcol[l, 1])).astype(BF16)
+        ahead = layer_loads(layers - 1)
+
+        @pl.when(l == 0)
+        def _():
+            for load in (*ahead[:3], load_dec):
+                load.start()
+
         scale = dim ** -0.5 * LOG2E
         s = scores(0)
         for hd in range(heads):
@@ -279,31 +275,43 @@
             o = mm(qkv[2 * part + hd * dim:2 * part + (hd + 1) * dim, :], p.astype(BF16))
             att[hd * dim:(hd + 1) * dim, :] = (o * (1.0 / total)).astype(BF16)
             s = nxt
+            if hd + 1 == heads // 2:
+                send_att[0].start()
+        send_att[1].start()
         load_o.wait()
-        copies = partials(0, l, att, wo, TN)
+        acc[:] = mm(att[:, mine], wo[feats, :], TN)
         pl.when(l > 0)(gather.relay_last)
-        add_partials(0, copies, row(6))
-        norm_rows(h, a, row(2), row(3), 64)
+        for copy in send_att:
+            copy.wait_recv()
+        r = acc[:] + mm(peer_att[:], wo[other_feats, :], TN)
+        rows = (h[mine, :].astype(F32) + r + row(6)).astype(BF16)
+        h[mine, :] = rows
+        low_a[:] = norm(rows.astype(F32), row(2), row(3)).astype(BF16)
+        for copy in send_att:
+            copy.wait_send()
+        pl.when(l == 0)(ahead[3].start)
         load_one.wait()
-        wide_bias = [vecs[l, pl.ds(8 + (hid // width) * core + i, 1), :] for i in range(hid // width)]
-        for j in range(hid // TOK):
+        for j in range(g.shape[1] // TOK):
             cols = slice(TOK * j, TOK * (j + 1))
             at = (TOK * j) % width
-            bias = wide_bias[(TOK * j) // width][:, at:at + TOK]
-            g[:, cols] = gelu(mm(a[:], w1[l, :, cols]) + bias).astype(BF16)
+            bias = row(8 + (TOK * j) // width)[:, at:at + TOK]
+            g[:, cols] = gelu(mm(low_a[:], w1[:, cols]) + bias).astype(BF16)
+        pl.when(l == 0)(ahead[4].start)
         pl.when(l == 0)(gather.relay)
         load_two.wait()
-        copies = partials(1, l, g, w2, NN)
-        add_partials(1, copies, row(7))
+        rows = (h[mine, :].astype(F32) + mm(g[:], w2[:]) + row(7)).astype(BF16)
+        h[mine, :] = rows
+        pl.when(l == 0)(ahead[5].start)
+        a[mine, :] = norm(rows.astype(F32), vecs[l + 1, 0:1, :], vecs[l + 1, 1:2, :]).astype(BF16)
+        send_rows.start()
+        get_rows.wait_recv()
+        send_rows.wait_send()
         return 0
 
+    norm_rows(h, a, vecs[0, 0:1, :], vecs[0, 1:2, :], 64)
     lax.fori_loop(0, layers, layer, 0)
-    norm_rows(h, a, fin[0:1, :], fin[1:2, :], 64)
     load_dec.wait()
     z_out[:] = mm(a[:], wdec[:]).astype(BF16)
-    for slot in range(2):
-        for copy in exchange(slot):
-            copy.wait_send()
     gather.finish()
     gather.drain()
     own.wait()
@@ -429,8 +437,8 @@
             copy.wait_send()
 
 
-def decoder_kernel(z, token, vec, fin, dall, w_qkv, w_o, w_one, w_two, y_out,
-                   wqkv, wo, w1, w2, dslots, h, a, own, aall, arecv, kt, vt, q, att, g, buf0, buf1, peak, tops, sums, outs, bcol,
+def decoder_kernel(token, vec, fin, z_in, dall, w_qkv, w_o, w_one, w_two, y_out,
+                   wqkv, wo, w1, w2, z, dslots, h, a, own, aall, arecv, kt, vt, q, att, g, buf0, buf1, peak, tops, sums, outs, bcol,
                    wsem, dsem, gsend, grecv):
     width = h.shape[1]
     layers = wqkv.shape[0]
@@ -440,8 +448,9 @@
     blocks = [pltpu.make_async_copy(dall.at[i], dslots.at[i], dsem.at[i]) for i in range(slots)]
     pairs = ((w_qkv, wqkv), (w_o, wo), (w_one, w1), (w_two, w2))
     loads = [[pltpu.make_async_copy(src.at[l], dst.at[l], wsem.at[l, i]) for i, (src, dst) in enumerate(pairs)] for l in range(layers)]
+    blocks.append(pltpu.make_async_copy(z_in, z, dsem.at[slots]))
     loads[0][0].start()
-    for block in blocks:
+    for block in reversed(blocks):
         block.start()
 
     for l in range(layers):
@@ -530,6 +539,7 @@
 
 VM = pl.BlockSpec(memory_space=pltpu.VMEM)
 HB = pl.BlockSpec(memory_space=pl.ANY)
+HBM = pl.BlockSpec(memory_space=pltpu.HBM)
 
 
 def solution(mesh):
@@ -547,34 +557,34 @@
         z, dall = pl.pallas_call(
             encoder_kernel,
             out_shape=(jax.ShapeDtypeStruct((TOK, DEC), BF16), jax.ShapeDtypeStruct((8, TOK, CODED), BF16)),
-            in_specs=[VM] * 7 + [HB] * 6,
+            in_specs=[VM] * 2 + [HB] * 11,
             out_specs=(VM, HB),
             scratch_shapes=[
-                vm(ALL, ENC),
-                vm(layers, 3 * PART, ENC), vm(layers, PART, ENC), vm(layers, ENC, HID), vm(layers, HID, ENC), vm(ENC, DEC), vmf(layers, 12, ENC),
+                vm(TOK, ALL), vm(TOK, ENC), vmf(12, layers, ENC), vmf(2, ENC), vm(ALL, ENC),
+                vm(3 * PART, ENC), vm(ENC, ENC), vm(ENC, 2 * HID), vm(2 * HID, ENC), vm(ENC, DEC), vmf(layers + 1, 12, ENC),
                 vm(chunks, 2, LANES, LANES), vm(*piece), vm(*piece), vm(*piece), vm(2, 2, *piece),
-                vm(TOK, ENC), vm(TOK, ENC), vm(3 * PART, TOK), vm(PART, TOK), vm(TOK, HID),
-                vmf(2, chunks, TOK, TOK), vmf(2, chunks, TOK, TOK), vm(TOK, CODED), vmf(layers, 2, PART, LANES),
-                dma((2,)), dma((layers, 6)), dma((chunks, chunks)), dma((chunks, chunks)), dma((2, chunks)), dma((2, chunks)), dma((9,)), dma((9,)), dma((1,)),
+                vm(TOK, ENC), vm(TOK, ENC), vm(LANES, ENC), vm(3 * PART, TOK), vm(PART, TOK), vm(PART, LANES), vmf(LANES, ENC), vm(LANES, 2 * HID),
+                vm(TOK, CODED), vmf(layers, 2, PART, LANES),
+                dma((6,)), dma((chunks,)), dma((layers, 6)), dma((chunks, chunks)), dma((chunks, chunks)), dma((4,)), dma((4,)), dma((9,)), dma((9,)), dma((1,)),
             ],
             compiler_params=pltpu.CompilerParams(collective_id=0, has_side_effects=True, vmem_limit_bytes=BIG),
             name="encoder",
-        )(patches, enc_pos, vis_mask.reshape(1, -1), dec_pos, b_embed, evec, enc_final, w_embed, ewqkv, ewo, enc_w1, enc_w2, w_dec_in)
+        )(vis_mask.reshape(1, -1), b_embed, patches, enc_pos, dec_pos, evec, enc_final, w_embed, ewqkv, ewo, enc_w1, enc_w2, w_dec_in)
         y = pl.pallas_call(
             decoder_kernel,
             out_shape=jax.ShapeDtypeStruct((TOK, DEC), BF16),
-            in_specs=[VM] * 4 + [HB] * 5,
+            in_specs=[VM] * 3 + [HBM] * 2 + [HB] * 4,
             out_specs=VM,
             scratch_shapes=[
                 vm(layers, ALL, DEC), vm(layers, DEC, DEC), vm(layers, DEC, KEYS), vm(layers, KEYS, DEC),
-                vm(8, TOK, CODED), vm(TOK, DEC), vm(TOK, DEC), vm(TOK, DEC), vm(8, TOK, DEC), vm(8, TOK, DEC),
+                vm(TOK, DEC), vm(8, TOK, CODED), vm(TOK, DEC), vm(TOK, DEC), vm(TOK, DEC), vm(8, TOK, DEC), vm(8, TOK, DEC),
                 vm(TERMS * DEC, KEYS), vm(DEC, KEYS), vm(TERMS * DEC, TOK), vm(DEC, TOK), vm(TOK, KEYS),
                 vmf(WIDE * TOK, TOK), vmf(WIDE * TOK, TOK), vmf(WIDE, 8, TOK), vmf(16, 8, TOK), vmf(16, 8, TOK), vmf(DEC, TOK), vmf(layers, 2, DEC, LANES),
-                dma((layers, 4)), dma((8,)), dma((14,)), dma((14,)),
+                dma((layers, 4)), dma((9,)), dma((14,)), dma((14,)),
             ],
             compiler_params=pltpu.CompilerParams(collective_id=1, has_side_effects=True, vmem_limit_bytes=MID),
             name="decoder",
-        )(z, mask_token, dvec, dec_final, dall, dwqkv, dwo, dec_w1, dec_w2)
+        )(mask_token, dvec, dec_final, z, dall, dwqkv, dwo, dec_w1, dec_w2)
         return jnp.dot(y, w_out, preferred_element_type=F32)
 
     token_rows = P(TOKEN_AXES, None)

time: 86.8 us -> 82.9 us (0.955)
  Pallas kernels: 83.9 us -> 80 us
    pallas_call x1, Pallas kernels: 45.6 us -> 41.7 us  [local_step(): pl.pallas_call(encoder_kernel, out_shape=(jax.ShapeDtypeStruct((TOK, DEC)...]
where the time goes in v4:
time: 82.9 us; the launch traced here: 82.7 us
  Pallas kernels  80 us (97%)
  matrix products  2.67 us (3%)
    pallas_call x1, Pallas kernels, local_step(): pl.pallas_call(encoder_kernel, out_shape=(jax.ShapeDtypeStruct((TOK, DEC)...  41.7 us
    pallas_call x1, Pallas kernels, local_step(): pl.pallas_call(decoder_kernel, out_shape=jax.ShapeDtypeStruct((TOK, DEC),...  38.3 us
    dot_general x1, matrix products, local_step(): return jnp.dot(y, w_out, preferred_element_type=F32)  2.67 us

profile of v4, /device:TPU:0, one launch (start us, length us, event | category | flops | bytes accessed | tf_op | source)
XLA Modules:
  0.0 82.7 jit_solution(13456354832842904910)
XLA Ops:
  0.0 41.7 %encoder.1 = (bf16[256,512]{1,0:T(8,128)(2,1)}, bf16[8,256,640]{2,1,0:T(8,128)(2,1)}) custom-call(s32[1,256]{1,0:T(1,128)} %bitcast.19, f32[1280]{0:T(1024)} %b_embed.1, bf16[256,1536]{1,0:T(8,128)(2,1)} %patches_in.1, bf16[256,1280]{1,0:T(8,128)(2,1)} %enc_pos_in.1, bf16[256,512]{1,0:T(8,128)(2,1)} %dec_pos.1, f32[12,2,1280]{2,1,0:T(2,128)} %bitcast.17, ...), custom_call_target="tpu_custom_call" | custom-call | tf_op jit(solution)/shard_map/encoder/pallas_call | solution.py:557
  41.7 0.0 copy-start
  41.7 38.3 %decoder.1 = bf16[256,512]{1,0:T(8,128)(2,1)} custom-call(bf16[512]{0:T(512)(128)(2,1)} %token_.1, f32[12,2,512]{2,1,0:T(2,128)} %bitcast.18, f32[2,512]{1,0:T(2,128)} %fin.1, bf16[256,512]{1,0:T(8,128)(2,1)} %get-tuple-element.7.z_in, bf16[8,256,640]{2,1,0:T(8,128)(2,1)} %get-tuple-element.8.dall, bf16[2,1536,512]{2,1,0:T(8,128)(2,1)} %bitcast.15, ...), custom_call_target="tpu_custom_call" | custom-call | tf_op jit(solution)/shard_map/decoder/pallas_call | solution.py:573
  80.0 0.0 copy-done
  80.0 2.7 %fusion = f32[256,1536]{1,0:T(8,128)} fusion(bf16[256,512]{1,0:T(8,128)(2,1)} %decoder.1, bf16[512,1536]{1,0:T(8,128)(2,1)S(1)} %copy-done), kind=kOutput, calls=%fused_computation | convolution fusion | flops 402653184 | bytes 3407872 | tf_op jit(solution)/shard_map/dot_general | solution.py:588
Async XLA Ops:
  41.7 38.3 %copy-start = (bf16[512,1536]{1,0:T(8,128)(2,1)S(1)}, bf16[512,1536]{1,0:T(8,128)(2,1)}, u32[]{:S(2)}) copy-start(bf16[512,1536]{1,0:T(8,128)(2,1)} %param.41) | copy-start | bytes 4718596

commit v5 on v4

--- a/solution.py
+++ b/solution.py
@@ -17,7 +17,7 @@
 NN = (((1,), (0,)), ((), ()))
 LOG2E = 1.4426950408889634
 TERMS, WIDE = 3, 16
-BIG, MID = 66_000_000, 65_000_000
+BIG, MID = 60_000_000, 50_000_000
 LANES, TOK, ENC, DEC = 128, 256, 1280, 512
 PART, HID, CODED, KEYS, ALL = 640, 2560, 640, 2048, 1536
 
@@ -61,9 +61,9 @@
 
 def neighbours():
     time, region = lax.axis_index("time"), lax.axis_index("region")
-    mate = {"batch": 0, "time": time, "region": region + 1 - 2 * (region % 2)}
-    across = {"batch": 0, "time": time, "region": (region + 2) % 4}
-    along = {"batch": 0, "time": 1 - time, "region": region}
+    mate = {"time": time, "region": region + 1 - 2 * (region % 2)}
+    across = {"time": time, "region": (region + 2) % 4}
+    along = {"time": 1 - time, "region": region}
     return mate, across, along
 
 
@@ -119,8 +119,8 @@
 
 
 def encoder_kernel(mask, b_embed, patches_in, enc_pos_in, dec_pos, vec_in, fin_in, w_embed, w_qkv, w_o, w_one, w_two, w_dec,
-                   z_out, dall,
-                   patches, enc_pos, vec, fin, wemb, wqkv, wo, w1, w2, wdec, vecs, ebuf, drecv, csum, xrecv, hb, h, a, low_a, qkv, att, peer_att, acc, g, dsrc, bcol,
+                   dall,
+                   zbuf, patches, enc_pos, vec, fin, wemb, wqkv, wo, w1, w2, wdec, vecs, ebuf, drecv, csum, xrecv, hb, h, a, low_a, qkv, att, peer_att, acc, g, dsrc, bcol,
                    wsem, esem, lsem, esend, erecv, xsend, xrecvs, gsend, grecv, osem):
     layers = w_qkv.shape[0]
     core = lax.axis_index("region") % 2
@@ -280,7 +280,6 @@
         send_att[1].start()
         load_o.wait()
         acc[:] = mm(att[:, mine], wo[feats, :], TN)
-        pl.when(l > 0)(gather.relay_last)
         for copy in send_att:
             copy.wait_recv()
         r = acc[:] + mm(peer_att[:], wo[other_feats, :], TN)
@@ -297,13 +296,14 @@
             bias = row(8 + (TOK * j) // width)[:, at:at + TOK]
             g[:, cols] = gelu(mm(low_a[:], w1[:, cols]) + bias).astype(BF16)
         pl.when(l == 0)(ahead[4].start)
-        pl.when(l == 0)(gather.relay)
+        pl.when(l > 0)(gather.relay_last)
         load_two.wait()
         rows = (h[mine, :].astype(F32) + mm(g[:], w2[:]) + row(7)).astype(BF16)
         h[mine, :] = rows
         pl.when(l == 0)(ahead[5].start)
         a[mine, :] = norm(rows.astype(F32), vecs[l + 1, 0:1, :], vecs[l + 1, 1:2, :]).astype(BF16)
         send_rows.start()
+        pl.when(l == 0)(gather.relay)
         get_rows.wait_recv()
         send_rows.wait_send()
         return 0
@@ -311,10 +311,13 @@
     norm_rows(h, a, vecs[0, 0:1, :], vecs[0, 1:2, :], 64)
     lax.fori_loop(0, layers, layer, 0)
     load_dec.wait()
-    z_out[:] = mm(a[:], wdec[:]).astype(BF16)
+    zbuf[:] = mm(a[:], wdec[:]).astype(BF16)
+    z_copy = pltpu.make_async_copy(zbuf, dall.at[8, :, pl.ds(0, DEC)], osem.at[1])
+    z_copy.start()
     gather.finish()
     gather.drain()
     own.wait()
+    z_copy.wait()
 
 
 def attend(q, kt, vt, att, buf, peak, state, dim, tiles, first, last, between=None):
@@ -437,7 +440,7 @@
             copy.wait_send()
 
 
-def decoder_kernel(token, vec, fin, z_in, dall, w_qkv, w_o, w_one, w_two, y_out,
+def decoder_kernel(token, vec, fin, dall, w_qkv, w_o, w_one, w_two, y_out,
                    wqkv, wo, w1, w2, z, dslots, h, a, own, aall, arecv, kt, vt, q, att, g, buf0, buf1, peak, tops, sums, outs, bcol,
                    wsem, dsem, gsend, grecv):
     width = h.shape[1]
@@ -448,7 +451,7 @@
     blocks = [pltpu.make_async_copy(dall.at[i], dslots.at[i], dsem.at[i]) for i in range(slots)]
     pairs = ((w_qkv, wqkv), (w_o, wo), (w_one, w1), (w_two, w2))
     loads = [[pltpu.make_async_copy(src.at[l], dst.at[l], wsem.at[l, i]) for i, (src, dst) in enumerate(pairs)] for l in range(layers)]
-    blocks.append(pltpu.make_async_copy(z_in, z, dsem.at[slots]))
+    blocks.append(pltpu.make_async_copy(dall.at[slots, :, pl.ds(0, DEC)], z, dsem.at[slots]))
     loads[0][0].start()
     for block in reversed(blocks):
         block.start()
@@ -496,10 +499,10 @@
         load.start()
     rows_in(0)
     queries(0, aall[0])
+    for i in range(1, slots):
+        rows_in(i)
     for i in range(slots):
         keys_values(0, i)
-        if i + 1 < slots:
-            rows_in(i + 1)
     attend(q, kt, vt, att, buf, peak, state, dim, range(slots), True, True)
     for load in loads[0][1:]:
         load.wait()
@@ -539,7 +542,6 @@
 
 VM = pl.BlockSpec(memory_space=pltpu.VMEM)
 HB = pl.BlockSpec(memory_space=pl.ANY)
-HBM = pl.BlockSpec(memory_space=pltpu.HBM)
 
 
 def solution(mesh):
@@ -554,18 +556,18 @@
         dma = pltpu.SemaphoreType.DMA
         chunks = ENC // TOK
         piece = (chunks, LANES, LANES)
-        z, dall = pl.pallas_call(
+        dall = pl.pallas_call(
             encoder_kernel,
-            out_shape=(jax.ShapeDtypeStruct((TOK, DEC), BF16), jax.ShapeDtypeStruct((8, TOK, CODED), BF16)),
+            out_shape=jax.ShapeDtypeStruct((LANES, TOK, CODED), BF16),
             in_specs=[VM] * 2 + [HB] * 11,
-            out_specs=(VM, HB),
+            out_specs=HB,
             scratch_shapes=[
-                vm(TOK, ALL), vm(TOK, ENC), vmf(12, layers, ENC), vmf(2, ENC), vm(ALL, ENC),
+                vm(TOK, DEC), vm(TOK, ALL), vm(TOK, ENC), vmf(12, layers, ENC), vmf(2, ENC), vm(ALL, ENC),
                 vm(3 * PART, ENC), vm(ENC, ENC), vm(ENC, 2 * HID), vm(2 * HID, ENC), vm(ENC, DEC), vmf(layers + 1, 12, ENC),
                 vm(chunks, 2, LANES, LANES), vm(*piece), vm(*piece), vm(*piece), vm(2, 2, *piece),
                 vm(TOK, ENC), vm(TOK, ENC), vm(LANES, ENC), vm(3 * PART, TOK), vm(PART, TOK), vm(PART, LANES), vmf(LANES, ENC), vm(LANES, 2 * HID),
                 vm(TOK, CODED), vmf(layers, 2, PART, LANES),
-                dma((6,)), dma((chunks,)), dma((layers, 6)), dma((chunks, chunks)), dma((chunks, chunks)), dma((4,)), dma((4,)), dma((9,)), dma((9,)), dma((1,)),
+                dma((6,)), dma((chunks,)), dma((layers, 6)), dma((chunks, chunks)), dma((chunks, chunks)), dma((4,)), dma((4,)), dma((9,)), dma((9,)), dma((2,)),
             ],
             compiler_params=pltpu.CompilerParams(collective_id=0, has_side_effects=True, vmem_limit_bytes=BIG),
             name="encoder",
@@ -573,7 +575,7 @@
         y = pl.pallas_call(
             decoder_kernel,
             out_shape=jax.ShapeDtypeStruct((TOK, DEC), BF16),
-            in_specs=[VM] * 3 + [HBM] * 2 + [HB] * 4,
+            in_specs=[VM] * 3 + [HB] * 5,
             out_specs=VM,
             scratch_shapes=[
                 vm(layers, ALL, DEC), vm(layers, DEC, DEC), vm(layers, DEC, KEYS), vm(layers, KEYS, DEC),
@@ -584,7 +586,7 @@
             ],
             compiler_params=pltpu.CompilerParams(collective_id=1, has_side_effects=True, vmem_limit_bytes=MID),
             name="decoder",
-        )(mask_token, dvec, dec_final, z, dall, dwqkv, dwo, dec_w1, dec_w2)
+        )(mask_token, dvec, dec_final, dall, dwqkv, dwo, dec_w1, dec_w2)
         return jnp.dot(y, w_out, preferred_element_type=F32)
 
     token_rows = P(TOKEN_AXES, None)

time: 82.9 us -> 77.9 us (0.940)
  Pallas kernels: 80 us -> 76 us
  matrix products: 2.67 us -> 1.73 us
    pallas_call x1, Pallas kernels: 38.3 us -> 34.8 us  [local_step(): pl.pallas_call(decoder_kernel, out_shape=jax.ShapeDtypeStruct((TOK, DEC),...]
    dot_general x1, matrix products: 2.67 us -> 1.73 us  [local_step(): return jnp.dot(y, w_out, preferred_element_type=F32)]
where the time goes in v5:
time: 77.9 us; the launch traced here: 77.8 us
  Pallas kernels  76 us (98%)
  matrix products  1.73 us (2%)
    pallas_call x1, Pallas kernels, local_step(): pl.pallas_call(encoder_kernel, out_shape=jax.ShapeDtypeStruct((LANES, TOK...  41.2 us
    pallas_call x1, Pallas kernels, local_step(): pl.pallas_call(decoder_kernel, out_shape=jax.ShapeDtypeStruct((TOK, DEC),...  34.8 us
    dot_general x1, matrix products, local_step(): return jnp.dot(y, w_out, preferred_element_type=F32)  1.73 us

profile of v5, /device:TPU:0, one launch (start us, length us, event | category | flops | bytes accessed | tf_op | source)
XLA Modules:
  0.0 77.8 jit_solution(1978999634127259696)
XLA Ops:
  0.0 0.0 copy-start
  0.0 0.0 copy-start.1
  0.0 0.0 copy-start.2
  0.0 0.0 copy-start.3
  0.0 0.0 copy-start.4
  0.0 0.0 copy-start.5
  0.0 41.2 %encoder.1.dall = bf16[128,256,640]{2,1,0:T(8,128)(2,1)} custom-call(s32[1,256]{1,0:T(1,128)} %bitcast.19, f32[1280]{0:T(1024)} %b_embed.1, bf16[256,1536]{1,0:T(8,128)(2,1)} %patches_in.1, bf16[256,1280]{1,0:T(8,128)(2,1)} %enc_pos_in.1, bf16[256,512]{1,0:T(8,128)(2,1)} %dec_pos.1, f32[12,2,1280]{2,1,0:T(2,128)} %bitcast.18, f32[2,1280]{1,0:T(2,128)} %fin_in.1, ...), custom_call_target="tpu_custom_call" | custom-call | tf_op jit(solution)/shard_map/encoder/pallas_call | solution.py:559
  41.2 0.0 copy-done.1
  41.2 0.0 copy-done.2
  41.2 0.0 copy-done.3
  41.2 0.0 copy-done.4
  41.2 0.0 copy-done.5
  41.2 34.8 %decoder.1 = bf16[256,512]{1,0:T(8,128)(2,1)S(1)} custom-call(bf16[512]{0:T(512)(128)(2,1)S(1)} %copy-done.5, f32[12,2,512]{2,1,0:T(2,128)S(1)} %bitcast.15, f32[2,512]{1,0:T(2,128)S(1)} %copy-done.4, bf16[128,256,640]{2,1,0:T(8,128)(2,1)} %encoder.1.dall, bf16[2,1536,512]{2,1,0:T(8,128)(2,1)S(1)} %bitcast.13, bf16[2,512,512]{2,1,0:T(8,128)(2,1)S(1)} %bitcast.14, ...), custom_call_target="tpu_custom_call" | custom-call | tf_op jit(solution)/shard_map/decoder/pallas_call | solution.py:575
  76.1 0.0 copy-done
  76.1 1.7 %fusion = f32[256,1536]{1,0:T(8,128)} fusion(bf16[256,512]{1,0:T(8,128)(2,1)S(1)} %decoder.1, bf16[512,1536]{1,0:T(8,128)(2,1)S(1)} %copy-done), kind=kOutput, calls=%fused_computation | convolution fusion | flops 402653184 | bytes 3407872 | tf_op jit(solution)/shard_map/dot_general | solution.py:590
Async XLA Ops:
  0.0 76.1 %copy-start = (bf16[512,1536]{1,0:T(8,128)(2,1)S(1)}, bf16[512,1536]{1,0:T(8,128)(2,1)}, u32[]{:S(2)}) copy-start(bf16[512,1536]{1,0:T(8,128)(2,1)} %param.41) | copy-start | bytes 4718596
  0.0 41.2 %copy-start.1 = (bf16[2,512,3,16,32]{1,4,3,2,0:T(8,128)(2,1)S(1)}, bf16[2,512,3,16,32]{1,4,3,2,0:T(8,128)(2,1)}, u32[]{:S(2)}) copy-start(bf16[2,512,3,16,32]{1,4,3,2,0:T(8,128)(2,1)} %param.36) | copy-start | bytes 9437188
  0.0 41.2 %copy-start.2 = (bf16[2,16,32,512]{3,2,1,0:T(8,128)(2,1)S(1)}, bf16[2,16,32,512]{3,2,1,0:T(8,128)(2,1)}, u32[]{:S(2)}) copy-start(bf16[2,16,32,512]{3,2,1,0:T(8,128)(2,1)} %param.37) | copy-start | bytes 3145732
  0.0 41.2 %copy-start.3 = (f32[2,12,512]{2,0,1:T(2,128)S(1)}, f32[2,12,512]{2,0,1:T(2,128)}, u32[]{:S(2)}) copy-start(f32[2,12,512]{2,0,1:T(2,128)} %param.35) | copy-start | bytes 147460
  0.0 41.2 %copy-start.4 = (f32[2,512]{1,0:T(2,128)S(1)}, f32[2,512]{1,0:T(2,128)}, u32[]{:S(2)}) copy-start(f32[2,512]{1,0:T(2,128)} %fin.1) | copy-start | bytes 12292
  0.0 41.2 %copy-start.5 = (bf16[512]{0:T(512)(128)(2,1)S(1)}, bf16[512]{0:T(512)(128)(2,1)}, u32[]{:S(2)}) copy-start(bf16[512]{0:T(512)(128)(2,1)} %token_.1) | copy-start | bytes 3076

commit v6 on v5

--- a/solution.py
+++ b/solution.py
@@ -16,6 +16,7 @@
 TN = (((0,), (0,)), ((), ()))
 NN = (((1,), (0,)), ((), ()))
 LOG2E = 1.4426950408889634
+GROUP = 2
 TERMS, WIDE = 3, 16
 BIG, MID = 60_000_000, 50_000_000
 LANES, TOK, ENC, DEC = 128, 256, 1280, 512
@@ -459,7 +460,7 @@
     for l in range(layers):
         bcol[l, 0] = column(vec[4, l:l + 1, :])
         bcol[l, 1] = column(vec[5, l:l + 1, :])
-    lane = lax.broadcasted_iota(jnp.int32, (TOK, LANES), 1).astype(F32) + 1.0
+    lane = lax.broadcasted_iota(jnp.int32, (GROUP * TOK, LANES), 1).astype(F32) + 1.0
     buf, state = (buf0, buf1), (tops, sums, outs)
 
     dim = width // 16
@@ -482,25 +483,25 @@
         vt[:, cols] = (mm(wqkv[l, 2 * width:, :], rows, NT) + twice(bcol[l, 1])).astype(BF16)
 
     def rows_in(i):
-        code = dslots[i, :, DEC:CODED].astype(F32)
+        wide = dslots[i:i + GROUP].reshape(-1, CODED)
+        code = wide[:, DEC:].astype(F32)
         pick = jnp.where(code == lane, 1.0, 0.0).astype(BF16)
         block = 0 if i < slots // 2 else LANES
         placed = mm(pick, z[block:block + LANES, :])
-        seen = code[:, 0:1] > 0.5
-        u = (jnp.where(seen, placed, token[:].astype(F32).reshape(1, -1)) + dslots[i, :, 0:DEC].astype(F32)).astype(BF16)
+        base = jnp.where(code[:, 0:1] > 0.5, placed, token[:].astype(F32).reshape(1, -1))
+        u = (base + wide[:, :DEC].astype(F32)).astype(BF16)
         if i == 0:
-            h[:] = u
-        aall[i] = norm(u.astype(F32), vec[0, 0:1, :], vec[1, 0:1, :]).astype(BF16)
+            h[:] = u[:TOK]
+        aall[i:i + GROUP] = norm(u.astype(F32), vec[0, 0:1, :], vec[1, 0:1, :]).astype(BF16).reshape(GROUP, TOK, DEC)
 
     for block in blocks:
         block.wait()
     loads[0][0].wait()
     for load in loads[0][1:] + loads[1]:
         load.start()
-    rows_in(0)
+    for i in range(0, slots, GROUP):
+        rows_in(i)
     queries(0, aall[0])
-    for i in range(1, slots):
-        rows_in(i)
     for i in range(slots):
         keys_values(0, i)
     attend(q, kt, vt, att, buf, peak, state, dim, range(slots), True, True)

time: 77.9 us -> 78 us (level)
  no operation moved by 1% of the time
where the time goes in v6:
time: 78 us; the launch traced here: 77.9 us
  Pallas kernels  76.1 us (98%)
  matrix products  1.73 us (2%)
    pallas_call x1, Pallas kernels, local_step(): pl.pallas_call(encoder_kernel, out_shape=jax.ShapeDtypeStruct((LANES, TOK...  41.2 us
    pallas_call x1, Pallas kernels, local_step(): pl.pallas_call(decoder_kernel, out_shape=jax.ShapeDtypeStruct((TOK, DEC),...  34.9 us
    dot_general x1, matrix products, local_step(): return jnp.dot(y, w_out, preferred_element_type=F32)  1.73 us

profile of v6, /device:TPU:0, one launch (start us, length us, event | category | flops | bytes accessed | tf_op | source)
XLA Modules:
  0.0 77.9 jit_solution(11980332243974332576)
XLA Ops:
  0.0 0.0 copy-start
  0.0 0.0 copy-start.1
  0.0 0.0 copy-start.2
  0.0 0.0 copy-start.3
  0.0 0.0 copy-start.4
  0.0 0.0 copy-start.5
  0.0 41.2 %encoder.1.dall = bf16[128,256,640]{2,1,0:T(8,128)(2,1)} custom-call(s32[1,256]{1,0:T(1,128)} %bitcast.19, f32[1280]{0:T(1024)} %b_embed.1, bf16[256,1536]{1,0:T(8,128)(2,1)} %patches_in.1, bf16[256,1280]{1,0:T(8,128)(2,1)} %enc_pos_in.1, bf16[256,512]{1,0:T(8,128)(2,1)} %dec_pos.1, f32[12,2,1280]{2,1,0:T(2,128)} %bitcast.18, f32[2,1280]{1,0:T(2,128)} %fin_in.1, ...), custom_call_target="tpu_custom_call" | custom-call | tf_op jit(solution)/shard_map/encoder/pallas_call | solution.py:560
  41.2 0.0 copy-done.1
  41.2 0.0 copy-done.2
  41.2 0.0 copy-done.3
  41.2 0.0 copy-done.4
  41.2 0.0 copy-done.5
  41.2 34.9 %decoder.1 = bf16[256,512]{1,0:T(8,128)(2,1)S(1)} custom-call(bf16[512]{0:T(512)(128)(2,1)S(1)} %copy-done.5, f32[12,2,512]{2,1,0:T(2,128)S(1)} %bitcast.15, f32[2,512]{1,0:T(2,128)S(1)} %copy-done.4, bf16[128,256,640]{2,1,0:T(8,128)(2,1)} %encoder.1.dall, bf16[2,1536,512]{2,1,0:T(8,128)(2,1)S(1)} %bitcast.13, bf16[2,512,512]{2,1,0:T(8,128)(2,1)S(1)} %bitcast.14, ...), custom_call_target="tpu_custom_call" | custom-call | tf_op jit(solution)/shard_map/decoder/pallas_call | solution.py:576
  76.2 0.0 copy-done
  76.2 1.7 %fusion = f32[256,1536]{1,0:T(8,128)} fusion(bf16[256,512]{1,0:T(8,128)(2,1)S(1)} %decoder.1, bf16[512,1536]{1,0:T(8,128)(2,1)S(1)} %copy-done), kind=kOutput, calls=%fused_computation | convolution fusion | flops 402653184 | bytes 3407872 | tf_op jit(solution)/shard_map/dot_general | solution.py:591
Async XLA Ops:
  0.0 76.2 %copy-start = (bf16[512,1536]{1,0:T(8,128)(2,1)S(1)}, bf16[512,1536]{1,0:T(8,128)(2,1)}, u32[]{:S(2)}) copy-start(bf16[512,1536]{1,0:T(8,128)(2,1)} %param.41) | copy-start | bytes 4718596
  0.0 41.2 %copy-start.1 = (bf16[2,512,3,16,32]{1,4,3,2,0:T(8,128)(2,1)S(1)}, bf16[2,512,3,16,32]{1,4,3,2,0:T(8,128)(2,1)}, u32[]{:S(2)}) copy-start(bf16[2,512,3,16,32]{1,4,3,2,0:T(8,128)(2,1)} %param.36) | copy-start | bytes 9437188
  0.0 41.2 %copy-start.2 = (bf16[2,16,32,512]{3,2,1,0:T(8,128)(2,1)S(1)}, bf16[2,16,32,512]{3,2,1,0:T(8,128)(2,1)}, u32[]{:S(2)}) copy-start(bf16[2,16,32,512]{3,2,1,0:T(8,128)(2,1)} %param.37) | copy-start | bytes 3145732
  0.0 41.2 %copy-start.3 = (f32[2,12,512]{2,0,1:T(2,128)S(1)}, f32[2,12,512]{2,0,1:T(2,128)}, u32[]{:S(2)}) copy-start(f32[2,12,512]{2,0,1:T(2,128)} %param.35) | copy-start | bytes 147460
  0.0 41.2 %copy-start.4 = (f32[2,512]{1,0:T(2,128)S(1)}, f32[2,512]{1,0:T(2,128)}, u32[]{:S(2)}) copy-start(f32[2,512]{1,0:T(2,128)} %fin.1) | copy-start | bytes 12292
  0.0 41.2 %copy-start.5 = (bf16[512]{0:T(512)(128)(2,1)S(1)}, bf16[512]{0:T(512)(128)(2,1)}, u32[]{:S(2)}) copy-start(bf16[512]{0:T(512)(128)(2,1)} %token_.1) | copy-start | bytes 3076
